TPU v7x, 32 devices: a whole 2x2x4 slice. The times are simulated.
32 devices in a mesh: groups: 2 (over y), seq: 4 (over z), mp: 2 (over x), sub: 2 (over core).
Axes of the slice: x: 2, y: 2, z: 4, core: 2. Of those that a mesh axis runs over, the one named last changes fastest.
Arguments:
- hidden_states: bfloat16 [2048, 8192], P(('groups', 'seq')), parts along dimension 0, may hold values from -8 to 8
- norm_gain: float32 [8192], replicated, may hold values from 0.25 to 1.75
- w_query: bfloat16 [8192, 2048], P('seq', ('mp', 'sub')), may hold values from -14 to 14
- w_keyval: bfloat16 [8192, 512], P('seq', ('mp', 'sub')), may hold values from -1 to 1
- doc_lengths: int32 [16], P('groups'), parts along dimension 0, may hold values from 1 to 512, 1024 in all
Outputs:
- attended: bfloat16 [2048, 2048], P(('groups', 'seq'), ('mp', 'sub')), parts along dimension 0
There are 2 independent parts, one for each index of `groups`. A program takes and returns all parts, laid end to end along the dimension named above; an argument that names none is the same for every part. Nothing has to cross between parts.
Inputs may be any that keep to these rules, and one draw needn't show every extreme that they name: `doc_lengths`: the lengths sum to 1024 and the longest is exactly 512.
All inputs are finite; a program needn't handle non-finite values.
Results may differ from a plain program's by a relative error of at most 0.0079.
Values may be sent and summed in bfloat16 or wider, within the bound.
No kernel may reach another device: no remote copies, remote signals or barrier semaphores. Data moves between devices by JAX's collectives and lax.ppermute only.
A program may use at most 64 MiB of HBM per device.

v0:
```python
import functools
import math

import jax
import jax.numpy as jnp
from jax import lax
from jax.experimental import pallas as pl
from jax.experimental.pallas import tpu as pltpu
from jax.sharding import PartitionSpec as P

HEAD_DIM = 128


NEG_LARGE = -1e30
ROPE_BASE = 500000.0
W_BOUND = 14.0
GAIN_BOUND = 1.75
WIRE_MAX = 60000.0


def inverse_norm(states):
    as_float = states.astype(jnp.float32)
    return lax.rsqrt(jnp.mean(as_float * as_float, axis=-1) + 1e-05)


def scaled(states, factor, gain):
    return (states.astype(jnp.float32) * factor[:, None] * gain[None, :]).astype(jnp.bfloat16)


def token_starts(positions, doc_lengths):
    doc_ends = jnp.cumsum(doc_lengths)
    begins = doc_ends - doc_lengths
    inside = begins[None, :] <= positions[:, None]
    return jnp.max(jnp.where(inside, begins[None, :], 0), axis=1)


def rope_tables(inner):
    half_dim = HEAD_DIM // 2
    frequency = jnp.exp(
        jnp.arange(half_dim, dtype=jnp.float32) * (-2.0 * math.log(ROPE_BASE) / HEAD_DIM)
    )
    angle = inner.astype(jnp.float32)[:, None] * frequency[None, :]
    cosine, sine = jnp.cos(angle), jnp.sin(angle)
    return (
        jnp.concatenate([cosine, cosine], axis=1),
        jnp.concatenate([-sine, sine], axis=1),
    )


def attend_kernel(
    reach, chunk, docs, scalars, query_ref, cos_ref, sin_ref, half_ref, other_ref, out_ref
):
    rows, count = query_ref.shape[0], half_ref.shape[0]
    heads = query_ref.shape[1] // HEAD_DIM
    first, is_key = scalars[0] * rows, scalars[1] == 0
    exponent_scale = math.log2(math.e) / math.sqrt(HEAD_DIM)
    column = first + lax.broadcasted_iota(jnp.int32, (rows, 1), 0)
    start = jnp.zeros((rows, 1), jnp.int32)
    begin = 0
    for k in range(docs):
        start = jnp.where(column >= begin, begin, start)
        begin = begin + scalars[2 + k]
    queries = []
    for h in range(heads):
        u = query_ref[:, h * HEAD_DIM : (h + 1) * HEAD_DIM]
        turned = pltpu.roll(u, HEAD_DIM // 2, 1)
        queries.append((u * cos_ref[...] + turned * sin_ref[...]).astype(jnp.bfloat16))
    for a in range(0, rows, chunk):
        low = (a + 1) // 128 * 128
        high = min(count, -(-(reach * rows + a + chunk) // 128) * 128)
        shape = (chunk, high - low)
        position = first + a + lax.broadcasted_iota(jnp.int32, shape, 0)
        key_position = first - reach * rows + low + lax.broadcasted_iota(jnp.int32, shape, 1)
        allowed = (key_position >= start[a : a + chunk]) & (key_position <= position)
        allowed = jnp.concatenate([allowed] * heads, axis=0)
        keys = jnp.where(is_key, half_ref[low:high, :], other_ref[low:high, :])
        values = jnp.where(is_key, other_ref[low:high, :], half_ref[low:high, :])
        query = jnp.concatenate([q[a : a + chunk] for q in queries], axis=0)
        scores = lax.dot_general(
            query, keys, (((1,), (1,)), ((), ())), preferred_element_type=jnp.float32
        )
        scores = jnp.where(allowed, scores, NEG_LARGE)
        top = jnp.max(scores, axis=-1, keepdims=True)
        weights = jnp.where(allowed, jnp.exp2((scores - top) * exponent_scale), 0.0)
        total = jnp.sum(weights, axis=-1, keepdims=True)
        summed = jnp.dot(weights.astype(jnp.bfloat16), values, preferred_element_type=jnp.float32)
        result = (summed / total).astype(jnp.bfloat16)
        for h in range(heads):
            columns = slice(h * HEAD_DIM, (h + 1) * HEAD_DIM)
            out_ref[a : a + chunk, columns] = result[h * chunk : (h + 1) * chunk]


def attend(reach, docs, scalars, query_sum, cosine, sine, half, other):
    rows, columns = query_sum.shape
    count = half.shape[0]
    chunk = rows
    while chunk > 16 and chunk * columns // HEAD_DIM * count > (1 << 19):
        chunk //= 2
    return pl.pallas_call(
        functools.partial(attend_kernel, reach, chunk, docs),
        out_shape=jax.ShapeDtypeStruct(query_sum.shape, jnp.bfloat16),
        in_specs=[pl.BlockSpec(memory_space=pltpu.SMEM)]
        + [pl.BlockSpec(memory_space=pltpu.VMEM)] * 5,
        out_specs=pl.BlockSpec(memory_space=pltpu.VMEM),
        cost_estimate=pl.CostEstimate(
            flops=4 * rows * count * columns,
            bytes_accessed=8 * rows * columns + 4 * count * HEAD_DIM,
            transcendentals=rows * count * columns // HEAD_DIM,
        ),
        name="attend",
    )(scalars, query_sum, cosine, sine, half, other)


def pull(array, axis, shift, size):
    pairs = [((i + shift) % size, i) for i in range(size)]
    return lax.ppermute(array, axis, pairs)


def dot(a, b):
    return jnp.dot(a, b, preferred_element_type=jnp.float32)


def stages_of(n):
    return [sorted({d, n - d}) for d in range(1, n // 2 + 1)]


def shards(sizes, hidden_states, norm_gain, w_query, w_keyval, doc_lengths):
    n, m_size, c_size = sizes["seq"], sizes["mp"], sizes["sub"]
    quarters = m_size * c_size
    row_count, width = hidden_states.shape
    depth = w_query.shape[0]
    piece = depth // quarters
    s, m, c = lax.axis_index("seq"), lax.axis_index("mp"), lax.axis_index("sub")
    stages = stages_of(n)

    bound = GAIN_BOUND * math.sqrt(width) * W_BOUND * math.sqrt(depth)
    wire_scale = 2.0 ** min(0, math.floor(math.log2(WIRE_MAX / bound)))
    unscale = 1.0 / wire_scale

    quarter = m * c_size + c
    arrived = {}
    for stage in stages:
        for d in stage:
            column = lax.rem(s + d, n) * depth + quarter * piece
            mine = lax.dynamic_slice_in_dim(hidden_states, column, piece, 1)
            arrived[d] = pull(mine, "seq", -d, n)
    factor = inverse_norm(hidden_states)
    factors = {d: pull(factor, "seq", -d, n) for stage in stages for d in stage}
    own = scaled(
        lax.dynamic_slice_in_dim(hidden_states, s * depth, depth, 1),
        factor,
        lax.dynamic_slice_in_dim(norm_gain, s * depth, depth, 0),
    )
    gain_piece = lax.dynamic_slice_in_dim(norm_gain, s * depth + quarter * piece, piece, 0)

    positions = s * row_count + jnp.arange(row_count, dtype=jnp.int32)
    starts = token_starts(positions, doc_lengths)
    cosine, sine = rope_tables(positions - starts)
    scalars = jnp.concatenate([jnp.stack([s, c]).astype(jnp.int32), doc_lengths])

    turned = []
    for j in range(c_size):
        for i in range(m_size):
            place = lax.rem(m + i, m_size) * c_size + lax.rem(c + j, c_size)
            rows = place * piece
            turned.append((lax.dynamic_slice_in_dim(w_query, rows, piece, 0),
                           lax.dynamic_slice_in_dim(w_keyval, rows, piece, 0)))
    step = m_size * piece
    wq_turned = jnp.concatenate([q for q, _ in turned], axis=0)
    wkv_turned = jnp.concatenate([kv for _, kv in turned], axis=0)
    keyval_sum = dot(own, w_keyval)
    query_sum = dot(own, w_query)
    q_parts, kv_parts = [], []
    for k, stage in enumerate(stages):
        for d in stage if k else []:
            arrived[d], _ = lax.optimization_barrier((arrived[d], first))
        first = jnp.concatenate([scaled(arrived[d], factors[d], gain_piece) for d in stage], axis=0)
        near = [first] + [pull(first, "mp", i, m_size) for i in range(1, m_size)]
        near = jnp.concatenate(near, axis=1)
        block = [near] + [pull(near, "sub", j, c_size) for j in range(1, c_size)]
        kvs, qs = [], []
        for i in range(len(stage)):
            parts = [b[i * row_count : (i + 1) * row_count] for b in block]
            rows = [slice(j * step, (j + 1) * step) for j in range(c_size)]
            kv_part = sum(dot(part, wkv_turned[r]) for part, r in zip(parts, rows))
            q_part = sum(dot(part, wq_turned[r]) for part, r in zip(parts, rows))
            kvs.append((kv_part * wire_scale).astype(jnp.float16))
            qs.append((q_part * wire_scale).astype(jnp.float16))
        kv_parts += [pull(part, "seq", d, n) for d, part in zip(stage, kvs)]
        q_parts += [pull(part, "seq", d, n) for d, part in zip(stage, qs)]
    for part in kv_parts:
        keyval_sum = keyval_sum + part.astype(jnp.float32) * unscale
    for part in q_parts:
        query_sum = query_sum + part.astype(jnp.float32) * unscale

    swapped = jnp.concatenate(
        [keyval_sum[:, HEAD_DIM // 2 :], keyval_sum[:, : HEAD_DIM // 2]], axis=1
    )
    rotated = keyval_sum * cosine + swapped * sine
    own_half = jnp.where(c == 0, rotated, keyval_sum).astype(jnp.bfloat16)
    reach = n // 2
    halves = []
    for e in range(reach, 0, -1):
        halves.append(lax.ppermute(own_half, "seq", [(i, i + e) for i in range(n - e)]))
    half = jnp.concatenate(halves + [own_half], axis=0)
    other = pull(half, "sub", 1, c_size)
    docs = doc_lengths.shape[0]
    return attend(reach, docs, scalars, query_sum, cosine, sine, half, other)


def solution(mesh):
    in_specs = (
        P(("groups", "seq"), None),
        P(),
        P("seq", ("mp", "sub")),
        P("seq", ("mp", "sub")),
        P("groups"),
    )
    out_specs = P(("groups", "seq"), ("mp", "sub"))
    sizes = dict(mesh.shape)

    def body(*arrays):
        return shards(sizes, *arrays)

    return jax.shard_map(body, mesh=mesh, in_specs=in_specs, out_specs=out_specs, check_vma=False)
```

profile of v0, /device:TPU:0, one launch (start us, length us, event | category | flops | bytes accessed | tf_op | source)
XLA Modules:
  0.0 99.1 jit_solution(900303878461562617)
XLA Ops:
  0.0 3.3 %multiply_reduce_fusion = f32[256]{0:T(256)S(1)} fusion(bf16[256,8192]{1,0:T(8,128)(2,1)} %param.5), kind=kLoop, calls=%fused_computation | loop fusion | flops 6291200 | bytes 4195328 | tf_op jit(solution)/shard_map/reduce_sum | solution.py:23
  3.3 3.1 %collective-permute-start.1 = (f32[256]{0:T(256)S(1)}, f32[256]{0:T(256)S(1)}, u32[]{:S(2)}, u32[]{:S(2)}) collective-permute-start(f32[256]{0:T(256)S(1)} %add_rsqrt_fusion), channel_id=1, source_target_pairs={{12,0},{0,4},{4,8},{8,12},{13,1},{1,5},{5,9},{9,13},{14,2},{2,6},{... | collective-permute-start | bytes 3080 | tf_op jit(solution)/shard_map/ppermute | solution.py:116
  6.4 2.1 %collective-permute-start.3 = (f32[256]{0:T(256)S(1)}, f32[256]{0:T(256)S(1)}, u32[]{:S(2)}, u32[]{:S(2)}) collective-permute-start(f32[256]{0:T(256)S(1)} %add_rsqrt_fusion), channel_id=1, source_target_pairs={{4,0},{8,4},{12,8},{0,12},{5,1},{9,5},{13,9},{1,13},{6,2},{10,6},{... | collective-permute-start | bytes 3080 | tf_op jit(solution)/shard_map/ppermute | solution.py:116
  9.4 1.2 %constant_dynamic-slice_fusion.10 = (bf16[256,512]{1,0:T(8,128)(2,1)S(1)}, bf16[256,512]{1,0:T(8,128)(2,1)S(1)}, bf16[256,512]{1,0:T(8,128)(2,1)S(1)}) fusion(bf16[256,8192]{1,0:T(8,128)(2,1)} %param.5, s32[]{:T(128)S(6)} %select_n.45, s32[]{:T(128)S(6)} %select_n.52, s32[]{:T(128)S(6)} %select_n.47), kind=kLoop, calls=%fused_computation.70 | loop fusion | bytes 1572876 | tf_op jit(solution)/shard_map/dynamic_slice | solution.py:145
  10.6 1.6 %collective-permute-start = (bf16[256,512]{1,0:T(8,128)(2,1)S(1)}, bf16[256,512]{1,0:T(8,128)(2,1)}, u32[]{:S(2)}, u32[]{:S(2)}) collective-permute-start(bf16[256,512]{1,0:T(8,128)(2,1)S(1)} %get-tuple-element.9), channel_id=1, source_target_pairs={{12,0},{0,4},{4,8},{8,12},{13,1},{1,5},{5,9},{9,13},{14,2},{2,6},{... | collective-permute-start | bytes 786440 | tf_op jit(solution)/shard_map/ppermute | solution.py:116
  12.2 2.2 %collective-permute-start.2 = (bf16[256,512]{1,0:T(8,128)(2,1)S(1)}, bf16[256,512]{1,0:T(8,128)(2,1)}, u32[]{:S(2)}, u32[]{:S(2)}) collective-permute-start(bf16[256,512]{1,0:T(8,128)(2,1)S(1)} %get-tuple-element.11), channel_id=1, source_target_pairs={{4,0},{8,4},{12,8},{0,12},{5,1},{9,5},{13,9},{1,13},{6,2},{10,6},{... | collective-permute-start | bytes 786440 | tf_op jit(solution)/shard_map/ppermute | solution.py:116
  15.3 2.0 %fusion.26 = f32[256,512]{1,0:T(8,128)S(1)} fusion(bf16[2048,512]{1,0:T(8,128)(2,1)S(1)} %copy-done, f32[2048]{0:T(1024)S(1)} %dynamic_slice.43, f32[256]{0:T(256)S(1)} %add_rsqrt_fusion, bf16[256,8192]{1,0:T(8,128)(2,1)} %param.5, s32[]{:T(128)S(6)} %select_n.44), kind=kOutput, calls=%fused_computation.48 | convolution fusion | flops 538968064 | bytes 3679236 | tf_op jit(solution)/shard_map/dot_general | solution.py:120
  18.4 3.4 %collective-permute-done = bf16[256,512]{1,0:T(8,128)(2,1)} collective-permute-done((bf16[256,512]{1,0:T(8,128)(2,1)S(1)}, bf16[256,512]{1,0:T(8,128)(2,1)}, u32[]{:S(2)}, u32[]{:S(2)}) %collective-permute-start) | collective-permute-done | bytes 262176 | tf_op jit(solution)/shard_map/ppermute | solution.py:116
  21.7 3.1 %collective-permute-done.2 = bf16[256,512]{1,0:T(8,128)(2,1)} collective-permute-done((bf16[256,512]{1,0:T(8,128)(2,1)S(1)}, bf16[256,512]{1,0:T(8,128)(2,1)}, u32[]{:S(2)}, u32[]{:S(2)}) %collective-permute-start.2) | collective-permute-done | bytes 262176 | tf_op jit(solution)/shard_map/ppermute | solution.py:116
  24.9 1.2 %multiply_convert_fusion.3 = (bf16[256,512]{1,0:T(8,128)(2,1)S(1)}, bf16[256,512]{1,0:T(8,128)(2,1)S(1)}) fusion(bf16[256,512]{1,0:T(8,128)(2,1)} %collective-permute-done, f32[512]{0:T(512)S(1)} %dynamic_slice.45, f32[256]{0:T(256)S(1)} %collective-permute-done.1, f32[256]{0:T(256)S(1)} %collective-permute-done.3, bf16[256,512]{1,0:T(8,128)(2,1)} %collective-permute-done.2), kind=kLoop, calls=%fused_computation.28 | loop fusion | flops 1048576 | bytes 1052672 | tf_op jit(solution)/shard_map/convert_element_type | solution.py:27
  26.9 9.6 %collective-permute-done.8 = bf16[256,512]{1,0:T(8,128)(2,1)S(1)} collective-permute-done((bf16[256,512]{1,0:T(8,128)(2,1)S(1)}, bf16[256,512]{1,0:T(8,128)(2,1)S(1)}, u32[]{:S(2)}, u32[]{:S(2)}) %collective-permute-start.8) | collective-permute-done | bytes 262176 | tf_op jit(solution)/shard_map/ppermute | solution.py:116
  36.6 1.6 %collective-permute-start.10 = (bf16[256,512]{1,0:T(8,128)(2,1)S(1)}, bf16[256,512]{1,0:T(8,128)(2,1)}, u32[]{:S(2)}, u32[]{:S(2)}) collective-permute-start(bf16[256,512]{1,0:T(8,128)(2,1)S(1)} %multiply_convert_fusion.1), channel_id=1, source_target_pairs={{2,0},{0,2},{3,1},{1,3},{6,4},{4,6},{7,5},{5,7},{10,8},{8,10},{11,... | collective-permute-start | bytes 786440 | tf_op jit(solution)/shard_map/ppermute | solution.py:116
  38.7 1.8 %fusion.31 = (f32[256,64]{1,0:T(8,128)S(1)}, f32[256,64]{1,0:T(8,128)}, f32[256,64]{1,0:T(8,128)}) fusion(f32[64]{0:T(128)} %multiply_exponential_fusion, f32[256]{0:T(256)S(1)} %subtract_convert_fusion), kind=kLoop, calls=%fused_computation.57 | loop fusion | flops 32768 | bytes 197888 | tf_op jit(solution)/shard_map/neg | solution.py:46
  41.1 4.9 %collective-permute-done.10 = bf16[256,512]{1,0:T(8,128)(2,1)} collective-permute-done((bf16[256,512]{1,0:T(8,128)(2,1)S(1)}, bf16[256,512]{1,0:T(8,128)(2,1)}, u32[]{:S(2)}, u32[]{:S(2)}) %collective-permute-start.10) | collective-permute-done | bytes 262176 | tf_op jit(solution)/shard_map/ppermute | solution.py:116
  46.0 1.8 %pad_maximum_fusion.4 = bf16[256,1024]{1,0:T(8,128)(2,1)} fusion(bf16[256,512]{1,0:T(8,128)(2,1)} %collective-permute-done.10, bf16[256,512]{1,0:T(8,128)(2,1)S(1)} %multiply_convert_fusion.1), kind=kLoop, calls=%fused_computation.24 | loop fusion | flops 1048576 | bytes 1048576 | tf_op jit(solution)/shard_map/concatenate | solution.py:179
  47.8 1.4 %constant_dynamic-slice_fusion.8 = (bf16[512,512]{1,0:T(8,128)(2,1)}, bf16[512,512]{1,0:T(8,128)(2,1)}, bf16[512,512]{1,0:T(8,128)(2,1)}, bf16[512,512]{1,0:T(8,128)(2,1)}) fusion(bf16[2048,512]{1,0:T(8,128)(2,1)S(1)} %copy-done, s32[]{:T(128)S(6)} %select_n.48, s32[]{:T(128)S(6)} %select_n.49, s32[]{:T(128)S(6)} %select_n.51, s32[]{:T(128)S(6)} %select_n.50), kind=kLoop, calls=%fused_computation.68 | loop fusion | bytes 4194320 | tf_op jit(solution)/shard_map/dynamic_slice | solution.py:166
  49.1 1.9 %fusion.25 = f32[256,128]{1,0:T(8,128)S(1)} fusion(bf16[2048,128]{1,0:T(8,128)(2,1)} %param.8, f32[2048]{0:T(1024)S(1)} %dynamic_slice.43, f32[256]{0:T(256)S(1)} %add_rsqrt_fusion, bf16[256,8192]{1,0:T(8,128)(2,1)} %param.5, s32[]{:T(128)S(6)} %select_n.44), kind=kOutput, calls=%fused_computation.47 | convolution fusion | flops 136314880 | bytes 1713156 | tf_op jit(solution)/shard_map/dot_general | solution.py:120
  51.1 5.2 %collective-permute-done.4 = bf16[512,512]{1,0:T(8,128)(2,1)} collective-permute-done((bf16[512,512]{1,0:T(8,128)(2,1)}, bf16[512,512]{1,0:T(8,128)(2,1)}, u32[]{:S(2)}, u32[]{:S(2)}) %collective-permute-start.4) | collective-permute-done | bytes 524320 | tf_op jit(solution)/shard_map/ppermute | solution.py:116
  56.3 1.1 %pad_maximum_fusion = bf16[512,1024]{1,0:T(8,128)(2,1)S(1)} fusion(bf16[512,512]{1,0:T(8,128)(2,1)} %collective-permute-done.4, bf16[256,512]{1,0:T(8,128)(2,1)S(1)} %get-tuple-element.24, bf16[256,512]{1,0:T(8,128)(2,1)S(1)} %get-tuple-element.23), kind=kLoop, calls=%fused_computation.20 | loop fusion | flops 3145728 | bytes 2097152 | tf_op jit(solution)/shard_map/concatenate | solution.py:179
  57.6 1.4 %fusion.30 = f32[256,128]{1,0:T(8,128)S(1)} fusion(bf16[256,1024]{1,0:T(8,128)(2,1)} %collective-permute-done.11, bf16[512,128]{1,0:T(8,128)(2,1)S(1)} %get-tuple-element.18, bf16[512,128]{1,0:T(8,128)(2,1)S(1)} %get-tuple-element.19), kind=kOutput, calls=%fused_computation.56 | convolution fusion | flops 67633152 | bytes 917504 | tf_op jit(solution)/shard_map/dot_general | solution.py:120
  59.0 1.3 %fusion.11 = f16[256,128]{1,0:T(8,128)(2,1)S(1)} fusion(f32[256,128]{1,0:T(8,128)S(1)} %fusion.30, bf16[512,128]{1,0:T(8,128)(2,1)S(1)} %get-tuple-element.17, bf16[512,128]{1,0:T(8,128)(2,1)S(1)} %get-tuple-element.16, bf16[256,512]{1,0:T(8,128)(2,1)} %collective-permute-done.10, bf16[256,512]{1,0:T(8,128)(2,1)S(1)} %multiply_convert_fusion.1), kind=kOutput, calls=%fused_computation.19 | convolution fusion | flops 68780032 | bytes 983040 | tf_op jit(solution)/shard_map/dot_general | solution.py:120
  60.5 1.5 %fusion.24 = f32[256,512]{1,0:T(8,128)S(1)} fusion(bf16[256,1024]{1,0:T(8,128)(2,1)} %collective-permute-done.11, bf16[512,512]{1,0:T(8,128)(2,1)S(1)} %copy-done.6, bf16[512,512]{1,0:T(8,128)(2,1)S(1)} %copy-done.7), kind=kOutput, calls=%fused_computation.41 | convolution fusion | flops 270532608 | bytes 2097152 | tf_op jit(solution)/shard_map/dot_general | solution.py:120
  62.0 1.4 %fusion.3 = f16[256,512]{1,0:T(8,128)(2,1)S(1)} fusion(f32[256,512]{1,0:T(8,128)S(1)} %fusion.24, bf16[512,512]{1,0:T(8,128)(2,1)S(1)} %copy-done.5, bf16[512,512]{1,0:T(8,128)(2,1)S(1)} %copy-done.4, bf16[256,512]{1,0:T(8,128)(2,1)} %collective-permute-done.10, bf16[256,512]{1,0:T(8,128)(2,1)S(1)} %multiply_convert_fusion.1), kind=kOutput, calls=%fused_computation.8 | convolution fusion | flops 271974400 | bytes 2359296 | tf_op jit(solution)/shard_map/dot_general | solution.py:120
  63.3 3.0 %collective-permute-start.12 = (f16[256,512]{1,0:T(8,128)(2,1)S(1)}, f16[256,512]{1,0:T(8,128)(2,1)S(1)}, u32[]{:S(2)}, u32[]{:S(2)}) collective-permute-start(f16[256,512]{1,0:T(8,128)(2,1)S(1)} %fusion.3), channel_id=1, source_target_pairs={{8,0},{12,4},{0,8},{4,12},{9,1},{13,5},{1,9},{5,13},{10,2},{14,6},... | collective-permute-start | bytes 786440 | tf_op jit(solution)/shard_map/ppermute | solution.py:116
  67.8 1.8 %collective-permute-start.14 = (f16[256,128]{1,0:T(8,128)(2,1)S(1)}, f16[256,128]{1,0:T(8,128)(2,1)S(1)}, u32[]{:S(2)}, u32[]{:S(2)}) collective-permute-start(f16[256,128]{1,0:T(8,128)(2,1)S(1)} %fusion.10), channel_id=1, source_target_pairs={{12,0},{0,4},{4,8},{8,12},{13,1},{1,5},{5,9},{9,13},{14,2},{2,6},{... | collective-permute-start | bytes 196616 | tf_op jit(solution)/shard_map/ppermute | solution.py:116
  70.5 2.1 %collective-permute-start.6 = (f16[256,512]{1,0:T(8,128)(2,1)S(1)}, f16[256,512]{1,0:T(8,128)(2,1)S(1)}, u32[]{:S(2)}, u32[]{:S(2)}) collective-permute-start(f16[256,512]{1,0:T(8,128)(2,1)S(1)} %fusion.5), channel_id=1, source_target_pairs={{4,0},{8,4},{12,8},{0,12},{5,1},{9,5},{13,9},{1,13},{6,2},{10,6},{... | collective-permute-start | bytes 786440 | tf_op jit(solution)/shard_map/ppermute | solution.py:116
  74.5 2.2 %collective-permute-done.14 = f16[256,128]{1,0:T(8,128)(2,1)S(1)} collective-permute-done((f16[256,128]{1,0:T(8,128)(2,1)S(1)}, f16[256,128]{1,0:T(8,128)(2,1)S(1)}, u32[]{:S(2)}, u32[]{:S(2)}) %collective-permute-start.14) | collective-permute-done | bytes 65568 | tf_op jit(solution)/shard_map/ppermute | solution.py:116
  77.7 12.2 %collective-permute-start.16 = (bf16[256,128]{1,0:T(8,128)(2,1)S(1)}, bf16[256,128]{1,0:T(8,128)(2,1)S(1)}, u32[]{:S(2)}, u32[]{:S(2)}) collective-permute-start(bf16[256,128]{1,0:T(8,128)(2,1)S(1)} %get-tuple-element.7), channel_id=1, source_target_pairs={{0,8},{4,12},{1,9},{5,13},{2,10},{6,14},{3,11},{7,15},{16,24},{20,... | collective-permute-start | bytes 196616 | tf_op jit(solution)/shard_map/ppermute | solution.py:204
  89.9 1.3 %collective-permute-start.17 = (bf16[256,128]{1,0:T(8,128)(2,1)S(1)}, bf16[256,128]{1,0:T(8,128)(2,1)S(1)}, u32[]{:S(2)}, u32[]{:S(2)}) collective-permute-start(bf16[256,128]{1,0:T(8,128)(2,1)S(1)} %get-tuple-element.7), channel_id=1, source_target_pairs={{0,4},{4,8},{8,12},{1,5},{5,9},{9,13},{2,6},{6,10},{10,14},{3,7},{... | collective-permute-start | bytes 196616 | tf_op jit(solution)/shard_map/ppermute | solution.py:204
  91.8 1.3 %collective-permute-done.17 = bf16[256,128]{1,0:T(8,128)(2,1)S(1)} collective-permute-done((bf16[256,128]{1,0:T(8,128)(2,1)S(1)}, bf16[256,128]{1,0:T(8,128)(2,1)S(1)}, u32[]{:S(2)}, u32[]{:S(2)}) %collective-permute-start.17) | collective-permute-done | bytes 65568 | tf_op jit(solution)/shard_map/ppermute | solution.py:204
  93.2 1.0 multiply_add_fusion.query_ref
  95.3 3.8 %attend.1 = bf16[256,512]{1,0:T(8,128)(2,1)} custom-call(s32[10]{0:T(128)} %pad_add_fusion.scalars, f32[256,512]{1,0:T(8,128)} %multiply_add_fusion.query_ref, f32[256,128]{1,0:T(8,128)} %get-tuple-element.20.cos_ref, f32[256,128]{1,0:T(8,128)} %get-tuple-element.8.sin_ref, bf16[768,128]{1,0:T(8,128)(2,1)} %copy-done.8, bf16[768,128]{1,0:T(8,128)(2,1)} %copy-done.11), custom_call_target="tpu_custom_call" | custom-call | flops 402653184 | bytes 1441792 | tf_op jit(solution)/shard_map/attend/pallas_call | solution.py:99
  (70 shorter events, 12.1 us)
Async XLA Ops:
  0.0 14.5 %copy-start.9 = (s32[8]{0:T(128)S(1)}, s32[8]{0:T(128)}, u32[]{:S(2)}) copy-start(s32[8]{0:T(128)} %param.9) | copy-start | bytes 100
  0.0 15.3 %copy-start = (bf16[2048,512]{1,0:T(8,128)(2,1)S(1)}, bf16[2048,512]{1,0:T(8,128)(2,1)}, u32[]{:S(2)}) copy-start(bf16[2048,512]{1,0:T(8,128)(2,1)} %param.7) | copy-start | bytes 6291460
  3.3 14.9 %collective-permute-start.1 = (f32[256]{0:T(256)S(1)}, f32[256]{0:T(256)S(1)}, u32[]{:S(2)}, u32[]{:S(2)}) collective-permute-start(f32[256]{0:T(256)S(1)} %add_rsqrt_fusion), channel_id=1, source_target_pairs={{12,0},{0,4},{4,8},{8,12},{13,1},{1,5},{5,9},{9,13},{14,2},{2,6},{... | collective-permute-start | bytes 3080 | tf_op jit(solution)/shard_map/ppermute | solution.py:116
  6.4 12.0 %collective-permute-start.3 = (f32[256]{0:T(256)S(1)}, f32[256]{0:T(256)S(1)}, u32[]{:S(2)}, u32[]{:S(2)}) collective-permute-start(f32[256]{0:T(256)S(1)} %add_rsqrt_fusion), channel_id=1, source_target_pairs={{4,0},{8,4},{12,8},{0,12},{5,1},{9,5},{13,9},{1,13},{6,2},{10,6},{... | collective-permute-start | bytes 3080 | tf_op jit(solution)/shard_map/ppermute | solution.py:116
  8.5 28.0 %collective-permute-start.9 = (f32[256]{0:T(256)S(1)}, f32[256]{0:T(256)S(1)}, u32[]{:S(2)}, u32[]{:S(2)}) collective-permute-start(f32[256]{0:T(256)S(1)} %add_rsqrt_fusion), channel_id=1, source_target_pairs={{8,0},{12,4},{0,8},{4,12},{9,1},{13,5},{1,9},{5,13},{10,2},{14,6},... | collective-permute-start | bytes 3080 | tf_op jit(solution)/shard_map/ppermute | solution.py:116
  10.6 11.2 %collective-permute-start = (bf16[256,512]{1,0:T(8,128)(2,1)S(1)}, bf16[256,512]{1,0:T(8,128)(2,1)}, u32[]{:S(2)}, u32[]{:S(2)}) collective-permute-start(bf16[256,512]{1,0:T(8,128)(2,1)S(1)} %get-tuple-element.9), channel_id=1, source_target_pairs={{12,0},{0,4},{4,8},{8,12},{13,1},{1,5},{5,9},{9,13},{14,2},{2,6},{... | collective-permute-start | bytes 786440 | tf_op jit(solution)/shard_map/ppermute | solution.py:116
  12.2 12.6 %collective-permute-start.2 = (bf16[256,512]{1,0:T(8,128)(2,1)S(1)}, bf16[256,512]{1,0:T(8,128)(2,1)}, u32[]{:S(2)}, u32[]{:S(2)}) collective-permute-start(bf16[256,512]{1,0:T(8,128)(2,1)S(1)} %get-tuple-element.11), channel_id=1, source_target_pairs={{4,0},{8,4},{12,8},{0,12},{5,1},{9,5},{13,9},{1,13},{6,2},{10,6},{... | collective-permute-start | bytes 786440 | tf_op jit(solution)/shard_map/ppermute | solution.py:116
  18.2 18.3 %collective-permute-start.8 = (bf16[256,512]{1,0:T(8,128)(2,1)S(1)}, bf16[256,512]{1,0:T(8,128)(2,1)S(1)}, u32[]{:S(2)}, u32[]{:S(2)}) collective-permute-start(bf16[256,512]{1,0:T(8,128)(2,1)S(1)} %get-tuple-element.10), channel_id=1, source_target_pairs={{8,0},{12,4},{0,8},{4,12},{9,1},{13,5},{1,9},{5,13},{10,2},{14,6},... | collective-permute-start | bytes 786440 | tf_op jit(solution)/shard_map/ppermute | solution.py:116
  36.6 9.3 %collective-permute-start.10 = (bf16[256,512]{1,0:T(8,128)(2,1)S(1)}, bf16[256,512]{1,0:T(8,128)(2,1)}, u32[]{:S(2)}, u32[]{:S(2)}) collective-permute-start(bf16[256,512]{1,0:T(8,128)(2,1)S(1)} %multiply_convert_fusion.1), channel_id=1, source_target_pairs={{2,0},{0,2},{3,1},{1,3},{6,4},{4,6},{7,5},{5,7},{10,8},{8,10},{11,... | collective-permute-start | bytes 786440 | tf_op jit(solution)/shard_map/ppermute | solution.py:116
  40.5 15.7 %collective-permute-start.4 = (bf16[512,512]{1,0:T(8,128)(2,1)}, bf16[512,512]{1,0:T(8,128)(2,1)}, u32[]{:S(2)}, u32[]{:S(2)}) collective-permute-start(bf16[512,512]{1,0:T(8,128)(2,1)} %pad_maximum_fusion.3), channel_id=1, source_target_pairs={{2,0},{0,2},{3,1},{1,3},{6,4},{4,6},{7,5},{5,7},{10,8},{8,10},{11,... | collective-permute-start | bytes 1572872 | tf_op jit(solution)/shard_map/ppermute | solution.py:116
  47.8 9.8 %collective-permute-start.11 = (bf16[256,1024]{1,0:T(8,128)(2,1)}, bf16[256,1024]{1,0:T(8,128)(2,1)}, u32[]{:S(2)}, u32[]{:S(2)}) collective-permute-start(bf16[256,1024]{1,0:T(8,128)(2,1)} %pad_maximum_fusion.4), channel_id=1, source_target_pairs={{1,0},{0,1},{3,2},{2,3},{5,4},{4,5},{7,6},{6,7},{9,8},{8,9},{11,10... | collective-permute-start | bytes 1572872 | tf_op jit(solution)/shard_map/ppermute | solution.py:116
  49.1 8.4 %copy-start.1 = (bf16[2048,128]{1,0:T(8,128)(2,1)S(1)}, bf16[2048,128]{1,0:T(8,128)(2,1)}, u32[]{:S(2)}) copy-start(bf16[2048,128]{1,0:T(8,128)(2,1)} %param.8) | copy-start | bytes 1572868
  57.4 3.0 %copy-start.6 = (bf16[512,512]{1,0:T(8,128)(2,1)S(1)}, bf16[512,512]{1,0:T(8,128)(2,1)}, u32[]{:S(2)}) copy-start(bf16[512,512]{1,0:T(8,128)(2,1)} %get-tuple-element.14) | copy-start | bytes 1572868
  57.4 3.0 %copy-start.7 = (bf16[512,512]{1,0:T(8,128)(2,1)S(1)}, bf16[512,512]{1,0:T(8,128)(2,1)}, u32[]{:S(2)}) copy-start(bf16[512,512]{1,0:T(8,128)(2,1)} %get-tuple-element.15) | copy-start | bytes 1572868
  57.4 8.9 %collective-permute-start.5 = (bf16[512,1024]{1,0:T(8,128)(2,1)S(1)}, bf16[512,1024]{1,0:T(8,128)(2,1)S(1)}, u32[]{:S(2)}, u32[]{:S(2)}) collective-permute-start(bf16[512,1024]{1,0:T(8,128)(2,1)S(1)} %pad_maximum_fusion), channel_id=1, source_target_pairs={{1,0},{0,1},{3,2},{2,3},{5,4},{4,5},{7,6},{6,7},{9,8},{8,9},{11,10... | collective-permute-start | bytes 3145736 | tf_op jit(solution)/shard_map/ppermute | solution.py:116
  59.0 2.9 %copy-start.4 = (bf16[512,512]{1,0:T(8,128)(2,1)S(1)}, bf16[512,512]{1,0:T(8,128)(2,1)}, u32[]{:S(2)}) copy-start(bf16[512,512]{1,0:T(8,128)(2,1)} %get-tuple-element.12) | copy-start | bytes 1572868
  59.0 2.9 %copy-start.5 = (bf16[512,512]{1,0:T(8,128)(2,1)S(1)}, bf16[512,512]{1,0:T(8,128)(2,1)}, u32[]{:S(2)}) copy-start(bf16[512,512]{1,0:T(8,128)(2,1)} %get-tuple-element.13) | copy-start | bytes 1572868
  60.4 13.2 %collective-permute-start.15 = (f16[256,128]{1,0:T(8,128)(2,1)S(1)}, f16[256,128]{1,0:T(8,128)(2,1)S(1)}, u32[]{:S(2)}, u32[]{:S(2)}) collective-permute-start(f16[256,128]{1,0:T(8,128)(2,1)S(1)} %fusion.11), channel_id=1, source_target_pairs={{8,0},{12,4},{0,8},{4,12},{9,1},{13,5},{1,9},{5,13},{10,2},{14,6},... | collective-permute-start | bytes 196616 | tf_op jit(solution)/shard_map/ppermute | solution.py:116
  63.3 29.9 %collective-permute-start.12 = (f16[256,512]{1,0:T(8,128)(2,1)S(1)}, f16[256,512]{1,0:T(8,128)(2,1)S(1)}, u32[]{:S(2)}, u32[]{:S(2)}) collective-permute-start(f16[256,512]{1,0:T(8,128)(2,1)S(1)} %fusion.3), channel_id=1, source_target_pairs={{8,0},{12,4},{0,8},{4,12},{9,1},{13,5},{1,9},{5,13},{10,2},{14,6},... | collective-permute-start | bytes 786440 | tf_op jit(solution)/shard_map/ppermute | solution.py:116
  66.9 7.6 %collective-permute-start.13 = (f16[256,128]{1,0:T(8,128)(2,1)S(1)}, f16[256,128]{1,0:T(8,128)(2,1)S(1)}, u32[]{:S(2)}, u32[]{:S(2)}) collective-permute-start(f16[256,128]{1,0:T(8,128)(2,1)S(1)} %fusion.9), channel_id=1, source_target_pairs={{4,0},{8,4},{12,8},{0,12},{5,1},{9,5},{13,9},{1,13},{6,2},{10,6},{... | collective-permute-start | bytes 196616 | tf_op jit(solution)/shard_map/ppermute | solution.py:116
  67.8 8.8 %collective-permute-start.14 = (f16[256,128]{1,0:T(8,128)(2,1)S(1)}, f16[256,128]{1,0:T(8,128)(2,1)S(1)}, u32[]{:S(2)}, u32[]{:S(2)}) collective-permute-start(f16[256,128]{1,0:T(8,128)(2,1)S(1)} %fusion.10), channel_id=1, source_target_pairs={{12,0},{0,4},{4,8},{8,12},{13,1},{1,5},{5,9},{9,13},{14,2},{2,6},{... | collective-permute-start | bytes 196616 | tf_op jit(solution)/shard_map/ppermute | solution.py:116
  70.5 22.7 %collective-permute-start.6 = (f16[256,512]{1,0:T(8,128)(2,1)S(1)}, f16[256,512]{1,0:T(8,128)(2,1)S(1)}, u32[]{:S(2)}, u32[]{:S(2)}) collective-permute-start(f16[256,512]{1,0:T(8,128)(2,1)S(1)} %fusion.5), channel_id=1, source_target_pairs={{4,0},{8,4},{12,8},{0,12},{5,1},{9,5},{13,9},{1,13},{6,2},{10,6},{... | collective-permute-start | bytes 786440 | tf_op jit(solution)/shard_map/ppermute | solution.py:116
  73.1 3.7 %copy-start.2 = (f32[256,64]{1,0:T(8,128)S(1)}, f32[256,64]{1,0:T(8,128)}, u32[]{:S(2)}) copy-start(f32[256,64]{1,0:T(8,128)} %get-tuple-element.26) | copy-start | bytes 196612
  73.1 3.7 %copy-start.3 = (f32[256,64]{1,0:T(8,128)S(1)}, f32[256,64]{1,0:T(8,128)}, u32[]{:S(2)}) copy-start(f32[256,64]{1,0:T(8,128)} %get-tuple-element.27) | copy-start | bytes 196612
  73.1 18.1 %copy-start.10 = (s32[8]{0:T(128)S(1)}, s32[8]{0:T(128)}, u32[]{:S(2)}) copy-start(s32[8]{0:T(128)} %param.9) | copy-start | bytes 100
  73.6 19.7 %collective-permute-start.7 = (f16[256,512]{1,0:T(8,128)(2,1)S(1)}, f16[256,512]{1,0:T(8,128)(2,1)S(1)}, u32[]{:S(2)}, u32[]{:S(2)}) collective-permute-start(f16[256,512]{1,0:T(8,128)(2,1)S(1)} %fusion.4), channel_id=1, source_target_pairs={{12,0},{0,4},{4,8},{8,12},{13,1},{1,5},{5,9},{9,13},{14,2},{2,6},{... | collective-permute-start | bytes 786440 | tf_op jit(solution)/shard_map/ppermute | solution.py:116
  77.7 14.1 %collective-permute-start.16 = (bf16[256,128]{1,0:T(8,128)(2,1)S(1)}, bf16[256,128]{1,0:T(8,128)(2,1)S(1)}, u32[]{:S(2)}, u32[]{:S(2)}) collective-permute-start(bf16[256,128]{1,0:T(8,128)(2,1)S(1)} %get-tuple-element.7), channel_id=1, source_target_pairs={{0,8},{4,12},{1,9},{5,13},{2,10},{6,14},{3,11},{7,15},{16,24},{20,... | collective-permute-start | bytes 196616 | tf_op jit(solution)/shard_map/ppermute | solution.py:204
  89.9 3.2 %collective-permute-start.17 = (bf16[256,128]{1,0:T(8,128)(2,1)S(1)}, bf16[256,128]{1,0:T(8,128)(2,1)S(1)}, u32[]{:S(2)}, u32[]{:S(2)}) collective-permute-start(bf16[256,128]{1,0:T(8,128)(2,1)S(1)} %get-tuple-element.7), channel_id=1, source_target_pairs={{0,4},{4,8},{8,12},{1,5},{5,9},{9,13},{2,6},{6,10},{10,14},{3,7},{... | collective-permute-start | bytes 196616 | tf_op jit(solution)/shard_map/ppermute | solution.py:204
  93.1 1.5 %copy-start.8 = (bf16[768,128]{1,0:T(8,128)(2,1)}, bf16[768,128]{1,0:T(8,128)(2,1)S(1)}, u32[]{:S(2)}) copy-start(bf16[768,128]{1,0:T(8,128)(2,1)S(1)} %pad_maximum_fusion.13.half_ref) | copy-start | bytes 589828
  93.1 1.5 %collective-permute-start.18 = (bf16[768,128]{1,0:T(8,128)(2,1)S(1)}, bf16[768,128]{1,0:T(8,128)(2,1)S(1)}, u32[]{:S(2)}, u32[]{:S(2)}) collective-permute-start(bf16[768,128]{1,0:T(8,128)(2,1)S(1)} %pad_maximum_fusion.13.half_ref), channel_id=1, source_target_pairs={{1,0},{0,1},{3,2},{2,3},{5,4},{4,5},{7,6},{6,7},{9,8},{8,9},{11,10... | collective-permute-start | bytes 589832 | tf_op jit(solution)/shard_map/ppermute | solution.py:116
  94.6 0.7 copy-start.11
where the time goes:
time: 99.7 us; the launch traced here: 99.1 us
  starting transfers between devices  33.3 us (33%)
  waiting for transfers between devices  30.9 us (31%)
  other arithmetic  13.6 us (14%)
  matrix products  12.4 us (12%)
  local copies, waits for them, and re-layouts  4.83 us (5%)
  Pallas kernels  3.81 us (4%)
    ppermute x17, waiting for transfers between devices, pull(): return lax.ppermute(array, axis, pairs)  29.6 us
    ppermute x17, starting transfers between devices, pull(): return lax.ppermute(array, axis, pairs)  19.8 us
    ppermute x2, starting transfers between devices, shards(): lax.ppermute(own_half, 'seq', [(i, i + e) for i in range(n - e)])  13.5 us
    dot_general x14, matrix products, dot(): return jnp.dot(a, b, preferred_element_type=jnp.float32)  12.4 us
    pallas_call x1, Pallas kernels, attend(): pl.pallas_call(functools.partial(attend_kernel, reach, chunk, docs), out_...  3.81 us
    reduce_sum x1, other arithmetic, inverse_norm(): return lax.rsqrt(jnp.mean(as_float * as_float, axis=-1) + 1e-05)  3.25 us
    concatenate x2, other arithmetic, shards(): near = jnp.concatenate(near, axis=1)  2.95 us
  transfers between devices with their start and end apart: 19, of which 9 were waited for; matrix products, arithmetic and copies ran while one was open for 27% of the time, Pallas kernels for 0%

commit v1 on v0

--- a/solution.py
+++ b/solution.py
@@ -16,15 +16,12 @@
 W_BOUND = 14.0
 GAIN_BOUND = 1.75
 WIRE_MAX = 60000.0
+KERNEL_VMEM = 16 << 20
 
 
 def inverse_norm(states):
     as_float = states.astype(jnp.float32)
     return lax.rsqrt(jnp.mean(as_float * as_float, axis=-1) + 1e-05)
-
-
-def scaled(states, factor, gain):
-    return (states.astype(jnp.float32) * factor[:, None] * gain[None, :]).astype(jnp.bfloat16)
 
 
 def token_starts(positions, doc_lengths):
@@ -107,6 +104,7 @@
             bytes_accessed=8 * rows * columns + 4 * count * HEAD_DIM,
             transcendentals=rows * count * columns // HEAD_DIM,
         ),
+        compiler_params=pltpu.CompilerParams(vmem_limit_bytes=KERNEL_VMEM),
         name="attend",
     )(scalars, query_sum, cosine, sine, half, other)
 
@@ -120,8 +118,54 @@
     return jnp.dot(a, b, preferred_element_type=jnp.float32)
 
 
-def stages_of(n):
-    return [sorted({d, n - d}) for d in range(1, n // 2 + 1)]
+def project_kernel(scale, count, places, factor_ref, gain_ref, wq_ref, wkv_ref, *refs):
+    pieces, (q_ref, kv_ref, block) = refs[:count], refs[count:]
+    for i, piece in enumerate(pieces):
+        for j in range(0, piece.shape[1], 128):
+            chosen = pl.ds(pl.multiple_of(places[i] + j, 128), 128)
+            part = piece[:, j : j + 128].astype(jnp.float32)
+            normed = part * factor_ref[...] * gain_ref[:, chosen]
+            block[:, chosen] = normed.astype(jnp.bfloat16)
+    kv_ref[...] = dot(block[...], wkv_ref[...]) * scale
+    q_ref[...] = dot(block[...], wq_ref[...]) * scale
+
+
+def project(pieces, places, factor, gain, w_query, w_keyval, scale):
+    rows, depth = pieces[0].shape[0], w_query.shape[0]
+    widths = [piece.shape[1] for piece in pieces]
+    columns = w_query.shape[1], w_keyval.shape[1]
+    if any(w % 128 for w in widths):
+        block = jnp.zeros((rows, depth), jnp.bfloat16)
+        for piece, place in zip(pieces, places):
+            block = lax.dynamic_update_slice_in_dim(block, piece, place, 1)
+        block = (block.astype(jnp.float32) * factor[:, None] * gain[None, :]).astype(jnp.bfloat16)
+        return dot(block, w_query) * scale, dot(block, w_keyval) * scale
+    in_vmem = pl.BlockSpec(memory_space=pltpu.VMEM)
+    return pl.pallas_call(
+        functools.partial(project_kernel, scale, len(pieces)),
+        out_shape=[jax.ShapeDtypeStruct((rows, w), jnp.float32) for w in columns],
+        in_specs=[pl.BlockSpec(memory_space=pltpu.SMEM)] + [in_vmem] * (4 + len(pieces)),
+        out_specs=[in_vmem, in_vmem],
+        scratch_shapes=[pltpu.VMEM((rows, depth), jnp.bfloat16)],
+        cost_estimate=pl.CostEstimate(
+            flops=2 * rows * depth * sum(columns),
+            bytes_accessed=2 * depth * sum(columns) + 2 * rows * depth,
+            transcendentals=0,
+        ),
+        compiler_params=pltpu.CompilerParams(vmem_limit_bytes=KERNEL_VMEM),
+        name="project",
+    )(
+        jnp.stack(places).astype(jnp.int32),
+        jnp.broadcast_to(factor[:, None], (rows, 128)),
+        gain[None, :],
+        w_query,
+        w_keyval,
+        *pieces,
+    )
+
+
+def offsets_of(n):
+    return sorted(range(1, n), key=lambda d: (min(d, n - d), d))
 
 
 def shards(sizes, hidden_states, norm_gain, w_query, w_keyval, doc_lengths):
@@ -131,7 +175,7 @@
     depth = w_query.shape[0]
     piece = depth // quarters
     s, m, c = lax.axis_index("seq"), lax.axis_index("mp"), lax.axis_index("sub")
-    stages = stages_of(n)
+    offsets = offsets_of(n)
 
     bound = GAIN_BOUND * math.sqrt(width) * W_BOUND * math.sqrt(depth)
     wire_scale = 2.0 ** min(0, math.floor(math.log2(WIRE_MAX / bound)))
@@ -139,55 +183,38 @@
 
     quarter = m * c_size + c
     arrived = {}
-    for stage in stages:
-        for d in stage:
-            column = lax.rem(s + d, n) * depth + quarter * piece
-            mine = lax.dynamic_slice_in_dim(hidden_states, column, piece, 1)
-            arrived[d] = pull(mine, "seq", -d, n)
+    for d in offsets:
+        column = lax.rem(s + d, n) * depth + quarter * piece
+        mine = lax.dynamic_slice_in_dim(hidden_states, column, piece, 1)
+        arrived[d] = pull(mine, "seq", -d, n)
     factor = inverse_norm(hidden_states)
-    factors = {d: pull(factor, "seq", -d, n) for stage in stages for d in stage}
-    own = scaled(
-        lax.dynamic_slice_in_dim(hidden_states, s * depth, depth, 1),
-        factor,
-        lax.dynamic_slice_in_dim(norm_gain, s * depth, depth, 0),
-    )
-    gain_piece = lax.dynamic_slice_in_dim(norm_gain, s * depth + quarter * piece, piece, 0)
+    factors = {d: pull(factor, "seq", -d, n) for d in offsets}
+    gain = lax.dynamic_slice_in_dim(norm_gain, s * depth, depth, 0)
 
     positions = s * row_count + jnp.arange(row_count, dtype=jnp.int32)
     starts = token_starts(positions, doc_lengths)
     cosine, sine = rope_tables(positions - starts)
     scalars = jnp.concatenate([jnp.stack([s, c]).astype(jnp.int32), doc_lengths])
 
-    turned = []
-    for j in range(c_size):
+    own = lax.dynamic_slice_in_dim(hidden_states, s * depth, depth, 1)
+    query_sum, keyval_sum = project(
+        [own], [jnp.zeros((), jnp.int32)], factor, gain, w_query, w_keyval, 1.0
+    )
+    places = [
+        (lax.rem(m + i, m_size) * c_size + lax.rem(c + j, c_size)) * piece
+        for i in range(m_size)
+        for j in range(c_size)
+    ]
+    q_parts, kv_parts = [], []
+    for d in offsets:
+        pieces = []
         for i in range(m_size):
-            place = lax.rem(m + i, m_size) * c_size + lax.rem(c + j, c_size)
-            rows = place * piece
-            turned.append((lax.dynamic_slice_in_dim(w_query, rows, piece, 0),
-                           lax.dynamic_slice_in_dim(w_keyval, rows, piece, 0)))
-    step = m_size * piece
-    wq_turned = jnp.concatenate([q for q, _ in turned], axis=0)
-    wkv_turned = jnp.concatenate([kv for _, kv in turned], axis=0)
-    keyval_sum = dot(own, w_keyval)
-    query_sum = dot(own, w_query)
-    q_parts, kv_parts = [], []
-    for k, stage in enumerate(stages):
-        for d in stage if k else []:
-            arrived[d], _ = lax.optimization_barrier((arrived[d], first))
-        first = jnp.concatenate([scaled(arrived[d], factors[d], gain_piece) for d in stage], axis=0)
-        near = [first] + [pull(first, "mp", i, m_size) for i in range(1, m_size)]
-        near = jnp.concatenate(near, axis=1)
-        block = [near] + [pull(near, "sub", j, c_size) for j in range(1, c_size)]
-        kvs, qs = [], []
-        for i in range(len(stage)):
-            parts = [b[i * row_count : (i + 1) * row_count] for b in block]
-            rows = [slice(j * step, (j + 1) * step) for j in range(c_size)]
-            kv_part = sum(dot(part, wkv_turned[r]) for part, r in zip(parts, rows))
-            q_part = sum(dot(part, wq_turned[r]) for part, r in zip(parts, rows))
-            kvs.append((kv_part * wire_scale).astype(jnp.float16))
-            qs.append((q_part * wire_scale).astype(jnp.float16))
-        kv_parts += [pull(part, "seq", d, n) for d, part in zip(stage, kvs)]
-        q_parts += [pull(part, "seq", d, n) for d, part in zip(stage, qs)]
+            near = pull(arrived[d], "mp", i, m_size) if i else arrived[d]
+            pieces += [near]
+            pieces += [pull(near, "sub", j, c_size) for j in range(1, c_size)]
+        q_part, kv_part = project(pieces, places, factors[d], gain, w_query, w_keyval, wire_scale)
+        kv_parts.append(pull(kv_part.astype(jnp.float16), "seq", d, n))
+        q_parts.append(pull(q_part.astype(jnp.float16), "seq", d, n))
     for part in kv_parts:
         keyval_sum = keyval_sum + part.astype(jnp.float32) * unscale
     for part in q_parts:

time: 99.7 us -> 102 us (1.023)
  the two profiles are of different devices: /device:TPU:0 before, /device:TPU:31 now
where the time goes in v1:
time: 102 us
  waiting for transfers between devices  43.4 us (43%)
  starting transfers between devices  24 us (24%)
  local copies, waits for them, and re-layouts  13.3 us (13%)
  Pallas kernels  12.1 us (12%)
  other arithmetic  8.67 us (8%)
    ppermute x2, waiting for transfers between devices, shards(): lax.ppermute(own_half, 'seq', [(i, i + e) for i in range(n - e)])  22.6 us
    ppermute x22, starting transfers between devices, pull(): return lax.ppermute(array, axis, pairs)  21.4 us
    ppermute x22, waiting for transfers between devices, pull(): return lax.ppermute(array, axis, pairs)  20.7 us
    pallas_call x4, Pallas kernels, project(): pl.pallas_call(functools.partial(project_kernel, scale, len(pieces)), out...  9.01 us
    unnamed x34, local copies, waits for them, and re-layouts  7.79 us
    pallas_call x1, Pallas kernels, attend(): pl.pallas_call(functools.partial(attend_kernel, reach, chunk, docs), out_...  3.12 us
    reduce_sum x1, other arithmetic, inverse_norm(): return lax.rsqrt(jnp.mean(as_float * as_float, axis=-1) + 1e-05)  3.1 us
    ppermute x2, starting transfers between devices, shards(): lax.ppermute(own_half, 'seq', [(i, i + e) for i in range(n - e)])  2.58 us
  transfers between devices with their start and end apart: 24, of which 6 were waited for; matrix products, arithmetic and copies ran while one was open for 12% of the time, Pallas kernels for 9%

profile of v1, /device:TPU:31, one launch (start us, length us, event | category | flops | bytes accessed | tf_op | source)
XLA Modules:
  0.0 101.8 jit_solution(7398065613712741317)
XLA Ops:
  0.0 2.1 %constant_dynamic-slice_fusion.2 = (bf16[256,512]{1,0:T(8,128)(2,1)S(1)}, bf16[256,512]{1,0:T(8,128)(2,1)}, bf16[256,512]{1,0:T(8,128)(2,1)}) fusion(bf16[256,8192]{1,0:T(8,128)(2,1)} %param.5, s32[]{:T(128)S(6)} %select_n.26, s32[]{:T(128)S(6)} %select_n.28, s32[]{:T(128)S(6)} %select_n.27), kind=kLoop, calls=%fused_computation.18 | loop fusion | bytes 1572876 | tf_op jit(solution)/shard_map/dynamic_slice | solution.py:188
  2.2 3.1 %multiply_reduce_fusion = f32[256]{0:T(256)S(1)} fusion(bf16[256,8192]{1,0:T(8,128)(2,1)} %param.5), kind=kLoop, calls=%fused_computation | loop fusion | flops 6291200 | bytes 4195328 | tf_op jit(solution)/shard_map/reduce_sum | solution.py:24
  5.3 1.3 %collective-permute-start = (f32[256]{0:T(256)S(1)}, f32[256]{0:T(256)S(1)}, u32[]{:S(2)}, u32[]{:S(2)}) collective-permute-start(f32[256]{0:T(256)S(1)} %add_rsqrt_fusion), channel_id=1, source_target_pairs={{12,0},{0,4},{4,8},{8,12},{13,1},{1,5},{5,9},{9,13},{14,2},{2,6},{... | collective-permute-start | bytes 3080 | tf_op jit(solution)/shard_map/ppermute | solution.py:114
  6.6 1.4 %collective-permute-start.13 = (bf16[256,512]{1,0:T(8,128)(2,1)}, bf16[256,512]{1,0:T(8,128)(2,1)}, u32[]{:S(2)}, u32[]{:S(2)}) collective-permute-start(bf16[256,512]{1,0:T(8,128)(2,1)} %get-tuple-element.24), channel_id=1, source_target_pairs={{8,0},{12,4},{0,8},{4,12},{9,1},{13,5},{1,9},{5,13},{10,2},{14,6},... | collective-permute-start | bytes 786440 | tf_op jit(solution)/shard_map/ppermute | solution.py:114
  8.3 2.3 %constant_dynamic-slice_fusion.3.refs_0_ = bf16[256,2048]{1,0:T(8,128)(2,1)} fusion(bf16[256,8192]{1,0:T(8,128)(2,1)} %param.5, s32[]{:T(128)S(6)} %select_n.25), kind=kLoop, calls=%fused_computation.19 | loop fusion | bytes 2097156 | tf_op jit(solution)/shard_map/dynamic_slice | solution.py:199
  10.9 2.1 %collective-permute-start.2 = (bf16[256,512]{1,0:T(8,128)(2,1)S(1)}, bf16[256,512]{1,0:T(8,128)(2,1)S(1)}, u32[]{:S(2)}, u32[]{:S(2)}) collective-permute-start(bf16[256,512]{1,0:T(8,128)(2,1)S(1)} %collective-permute-done.1.refs_0_), channel_id=1, source_target_pairs={{1,0},{0,1},{3,2},{2,3},{5,4},{4,5},{7,6},{6,7},{9,8},{8,9},{11,10... | collective-permute-start | bytes 786440 | tf_op jit(solution)/shard_map/ppermute | solution.py:114
  13.7 13.5 %collective-permute-done.13.refs_0_ = bf16[256,512]{1,0:T(8,128)(2,1)} collective-permute-done((bf16[256,512]{1,0:T(8,128)(2,1)}, bf16[256,512]{1,0:T(8,128)(2,1)}, u32[]{:S(2)}, u32[]{:S(2)}) %collective-permute-start.13) | collective-permute-done | bytes 262176 | tf_op jit(solution)/shard_map/ppermute | solution.py:114
  27.5 1.2 %collective-permute-start.9 = (bf16[256,512]{1,0:T(8,128)(2,1)S(1)}, bf16[256,512]{1,0:T(8,128)(2,1)}, u32[]{:S(2)}, u32[]{:S(2)}) collective-permute-start(bf16[256,512]{1,0:T(8,128)(2,1)S(1)} %collective-permute-done.7.refs_0_), channel_id=1, source_target_pairs={{2,0},{0,2},{3,1},{1,3},{6,4},{4,6},{7,5},{5,7},{10,8},{8,10},{11,... | collective-permute-start | bytes 786440 | tf_op jit(solution)/shard_map/ppermute | solution.py:114
  28.8 1.1 %collective-permute-start.4 = (bf16[256,512]{1,0:T(8,128)(2,1)S(1)}, bf16[256,512]{1,0:T(8,128)(2,1)}, u32[]{:S(2)}, u32[]{:S(2)}) collective-permute-start(bf16[256,512]{1,0:T(8,128)(2,1)S(1)} %collective-permute-done.3.refs_2_), channel_id=1, source_target_pairs={{1,0},{0,1},{3,2},{2,3},{5,4},{4,5},{7,6},{6,7},{9,8},{8,9},{11,10... | collective-permute-start | bytes 786440 | tf_op jit(solution)/shard_map/ppermute | solution.py:114
  31.8 3.0 %collective-permute-done.15.refs_2_ = bf16[256,512]{1,0:T(8,128)(2,1)} collective-permute-done((bf16[256,512]{1,0:T(8,128)(2,1)}, bf16[256,512]{1,0:T(8,128)(2,1)}, u32[]{:S(2)}, u32[]{:S(2)}) %collective-permute-start.15) | collective-permute-done | bytes 262176 | tf_op jit(solution)/shard_map/ppermute | solution.py:114
  34.9 2.4 %collective-permute-start.16 = (bf16[256,512]{1,0:T(8,128)(2,1)}, bf16[256,512]{1,0:T(8,128)(2,1)}, u32[]{:S(2)}, u32[]{:S(2)}) collective-permute-start(bf16[256,512]{1,0:T(8,128)(2,1)} %collective-permute-done.15.refs_2_), channel_id=1, source_target_pairs={{1,0},{0,1},{3,2},{2,3},{5,4},{4,5},{7,6},{6,7},{9,8},{8,9},{11,10... | collective-permute-start | bytes 786440 | tf_op jit(solution)/shard_map/ppermute | solution.py:114
  37.2 3.3 %collective-permute-done.9.refs_2_ = bf16[256,512]{1,0:T(8,128)(2,1)} collective-permute-done((bf16[256,512]{1,0:T(8,128)(2,1)S(1)}, bf16[256,512]{1,0:T(8,128)(2,1)}, u32[]{:S(2)}, u32[]{:S(2)}) %collective-permute-start.9) | collective-permute-done | bytes 262176 | tf_op jit(solution)/shard_map/ppermute | solution.py:114
  40.5 1.4 %collective-permute-start.10 = (bf16[256,512]{1,0:T(8,128)(2,1)}, bf16[256,512]{1,0:T(8,128)(2,1)}, u32[]{:S(2)}, u32[]{:S(2)}) collective-permute-start(bf16[256,512]{1,0:T(8,128)(2,1)} %collective-permute-done.9.refs_2_), channel_id=1, source_target_pairs={{1,0},{0,1},{3,2},{2,3},{5,4},{4,5},{7,6},{6,7},{9,8},{8,9},{11,10... | collective-permute-start | bytes 786440 | tf_op jit(solution)/shard_map/ppermute | solution.py:114
  44.3 0.9 copy-done.10
  45.3 0.9 copy-done.12
  46.2 2.4 %project.5 = (f32[256,512]{1,0:T(8,128)S(1)}, f32[256,128]{1,0:T(8,128)S(1)}) custom-call(s32[4]{0:T(128)S(1)} %pad_add_fusion.1.places, f32[256,128]{1,0:T(8,128)S(1)} %broadcast_in_dim.22.factor_ref, f32[1,2048]{1,0:T(1,128)S(1)} %bitcast.10, bf16[2048,512]{1,0:T(8,128)(2,1)S(1)} %copy-done, bf16[2048,128]{1,0:T(8,128)(2,1)S(1)} %copy-done.1, ...), custom_call_target="tpu_custom_call" | custom-call | flops 671088640 | bytes 3670016 | tf_op jit(solution)/shard_map/project/pallas_call | solution.py:144
  49.3 2.6 %collective-permute-start.18 = (f16[256,128]{1,0:T(8,128)(2,1)}, f16[256,128]{1,0:T(8,128)(2,1)}, u32[]{:S(2)}, u32[]{:S(2)}) collective-permute-start(f16[256,128]{1,0:T(8,128)(2,1)} %convert_element_type.57), channel_id=1, source_target_pairs={{4,0},{8,4},{12,8},{0,12},{5,1},{9,5},{13,9},{1,13},{6,2},{10,6},{... | collective-permute-start | bytes 196616 | tf_op jit(solution)/shard_map/ppermute | solution.py:114
  52.0 2.6 %project.7 = (f32[256,512]{1,0:T(8,128)S(1)}, f32[256,128]{1,0:T(8,128)S(1)}) custom-call(s32[4]{0:T(128)S(1)} %pad_add_fusion.1.places, f32[256,128]{1,0:T(8,128)S(1)} %broadcast_in_dim.24.factor_ref, f32[1,2048]{1,0:T(1,128)S(1)} %bitcast.11, bf16[2048,512]{1,0:T(8,128)(2,1)S(1)} %copy-done, bf16[2048,128]{1,0:T(8,128)(2,1)S(1)} %copy-done.1, ...), custom_call_target="tpu_custom_call" | custom-call | flops 671088640 | bytes 3670016 | tf_op jit(solution)/shard_map/project/pallas_call | solution.py:144
  57.1 2.6 %project.6 = (f32[256,512]{1,0:T(8,128)S(1)}, f32[256,128]{1,0:T(8,128)S(1)}) custom-call(s32[4]{0:T(128)S(1)} %pad_add_fusion.1.places, f32[256,128]{1,0:T(8,128)S(1)} %broadcast_in_dim.23.factor_ref, f32[1,2048]{1,0:T(1,128)S(1)} %bitcast.12, bf16[2048,512]{1,0:T(8,128)(2,1)S(1)} %copy-done, bf16[2048,128]{1,0:T(8,128)(2,1)S(1)} %copy-done.1, ...), custom_call_target="tpu_custom_call" | custom-call | flops 671088640 | bytes 3670016 | tf_op jit(solution)/shard_map/project/pallas_call | solution.py:144
  61.1 1.2 %collective-permute-start.19 = (f16[256,128]{1,0:T(8,128)(2,1)}, f16[256,128]{1,0:T(8,128)(2,1)}, u32[]{:S(2)}, u32[]{:S(2)}) collective-permute-start(f16[256,128]{1,0:T(8,128)(2,1)} %convert_element_type.59), channel_id=1, source_target_pairs={{12,0},{0,4},{4,8},{8,12},{13,1},{1,5},{5,9},{9,13},{14,2},{2,6},{... | collective-permute-start | bytes 196616 | tf_op jit(solution)/shard_map/ppermute | solution.py:114
  62.4 1.2 %fusion.3 = (f32[256,64]{1,0:T(8,128)S(1)}, f32[256,64]{1,0:T(8,128)S(1)}, f32[256,64]{1,0:T(8,128)}) fusion(f32[64]{0:T(128)S(1)} %copy-done.14, f32[256]{0:T(256)S(1)} %subtract_convert_fusion), kind=kLoop, calls=%fused_computation.12 | loop fusion | flops 32768 | bytes 197888 | tf_op jit(solution)/shard_map/neg | solution.py:43
  63.7 1.2 %copy-done.2 = bf16[256,2048]{1,0:T(8,128)(2,1)S(1)} copy-done((bf16[256,2048]{1,0:T(8,128)(2,1)S(1)}, bf16[256,2048]{1,0:T(8,128)(2,1)}, u32[]{:S(2)}) %copy-start.2) | copy-done | bytes 1048600
  64.9 1.4 %project.4 = (f32[256,512]{1,0:T(8,128)S(1)}, f32[256,128]{1,0:T(8,128)S(1)}) custom-call(s32[1]{0:T(128)} %constant.46.clone.1.places, f32[256,128]{1,0:T(8,128)S(1)} %broadcast_in_dim.20.factor_ref, f32[1,2048]{1,0:T(1,128)S(1)} %bitcast.13, bf16[2048,512]{1,0:T(8,128)(2,1)S(1)} %copy-done, bf16[2048,128]{1,0:T(8,128)(2,1)S(1)} %copy-done.1, ...), custom_call_target="tpu_custom_call" | custom-call | flops 671088640 | bytes 3670016 | tf_op jit(solution)/shard_map/project/pallas_call | solution.py:144
  66.7 1.5 %collective-permute-start.17 = (f16[256,512]{1,0:T(8,128)(2,1)S(1)}, f16[256,512]{1,0:T(8,128)(2,1)S(1)}, u32[]{:S(2)}, u32[]{:S(2)}) collective-permute-start(f16[256,512]{1,0:T(8,128)(2,1)S(1)} %convert_element_type.54), channel_id=1, source_target_pairs={{8,0},{12,4},{0,8},{4,12},{9,1},{13,5},{1,9},{5,13},{10,2},{14,6},... | collective-permute-start | bytes 786440 | tf_op jit(solution)/shard_map/ppermute | solution.py:114
  68.3 1.7 %collective-permute-start.11 = (f16[256,512]{1,0:T(8,128)(2,1)S(1)}, f16[256,512]{1,0:T(8,128)(2,1)S(1)}, u32[]{:S(2)}, u32[]{:S(2)}) collective-permute-start(f16[256,512]{1,0:T(8,128)(2,1)S(1)} %convert_element_type.52), channel_id=1, source_target_pairs={{12,0},{0,4},{4,8},{8,12},{13,1},{1,5},{5,9},{9,13},{14,2},{2,6},{... | collective-permute-start | bytes 786440 | tf_op jit(solution)/shard_map/ppermute | solution.py:114
  69.9 0.9 multiply_add_fusion.1
  71.2 1.3 %collective-permute-start.22 = (bf16[256,128]{1,0:T(8,128)(2,1)S(1)}, bf16[256,128]{1,0:T(8,128)(2,1)S(1)}, u32[]{:S(2)}, u32[]{:S(2)}) collective-permute-start(bf16[256,128]{1,0:T(8,128)(2,1)S(1)} %get-tuple-element.21), channel_id=1, source_target_pairs={{0,4},{4,8},{8,12},{1,5},{5,9},{9,13},{2,6},{6,10},{10,14},{3,7},{... | collective-permute-start | bytes 196616 | tf_op jit(solution)/shard_map/ppermute | solution.py:231
  72.5 1.3 %collective-permute-start.21 = (bf16[256,128]{1,0:T(8,128)(2,1)S(1)}, bf16[256,128]{1,0:T(8,128)(2,1)S(1)}, u32[]{:S(2)}, u32[]{:S(2)}) collective-permute-start(bf16[256,128]{1,0:T(8,128)(2,1)S(1)} %get-tuple-element.21), channel_id=1, source_target_pairs={{0,8},{4,12},{1,9},{5,13},{2,10},{6,14},{3,11},{7,15},{16,24},{20,... | collective-permute-start | bytes 196616 | tf_op jit(solution)/shard_map/ppermute | solution.py:231
  73.9 14.7 %collective-permute-done.22 = bf16[256,128]{1,0:T(8,128)(2,1)S(1)} collective-permute-done((bf16[256,128]{1,0:T(8,128)(2,1)S(1)}, bf16[256,128]{1,0:T(8,128)(2,1)S(1)}, u32[]{:S(2)}, u32[]{:S(2)}) %collective-permute-start.22) | collective-permute-done | bytes 65568 | tf_op jit(solution)/shard_map/ppermute | solution.py:231
  88.5 8.0 %collective-permute-done.21 = bf16[256,128]{1,0:T(8,128)(2,1)S(1)} collective-permute-done((bf16[256,128]{1,0:T(8,128)(2,1)S(1)}, bf16[256,128]{1,0:T(8,128)(2,1)S(1)}, u32[]{:S(2)}, u32[]{:S(2)}) %collective-permute-start.21) | collective-permute-done | bytes 65568 | tf_op jit(solution)/shard_map/ppermute | solution.py:231
  96.5 1.1 %collective-permute-start.23 = (bf16[768,128]{1,0:T(8,128)(2,1)S(1)}, bf16[768,128]{1,0:T(8,128)(2,1)S(1)}, u32[]{:S(2)}, u32[]{:S(2)}) collective-permute-start(bf16[768,128]{1,0:T(8,128)(2,1)S(1)} %pad_maximum_fusion.half_ref), channel_id=1, source_target_pairs={{1,0},{0,1},{3,2},{2,3},{5,4},{4,5},{7,6},{6,7},{9,8},{8,9},{11,10... | collective-permute-start | bytes 589832 | tf_op jit(solution)/shard_map/ppermute | solution.py:114
  98.7 3.1 %attend.1 = bf16[256,512]{1,0:T(8,128)(2,1)} custom-call(s32[10]{0:T(128)S(1)} %pad_add_fusion.scalars, f32[256,512]{1,0:T(8,128)S(1)} %multiply_add_fusion.query_ref, f32[256,128]{1,0:T(8,128)S(1)} %get-tuple-element.26.cos_ref, f32[256,128]{1,0:T(8,128)S(1)} %get-tuple-element.22.sin_ref, bf16[768,128]{1,0:T(8,128)(2,1)S(1)} %pad_maximum_fusion.half_ref, ...), custom_call_target="tpu_custom_call" | custom-call | flops 402653184 | bytes 1441792 | tf_op jit(solution)/shard_map/attend/pallas_call | solution.py:96
  (84 shorter events, 12.6 us)
Async XLA Ops:
  0.0 8.1 %copy-start.15 = (s32[8]{0:T(128)S(1)}, s32[8]{0:T(128)}, u32[]{:S(2)}) copy-start(s32[8]{0:T(128)} %param.9) | copy-start | bytes 100
  0.0 43.4 %copy-start.1 = (bf16[2048,128]{1,0:T(8,128)(2,1)S(1)}, bf16[2048,128]{1,0:T(8,128)(2,1)}, u32[]{:S(2)}) copy-start(bf16[2048,128]{1,0:T(8,128)(2,1)} %wkv_ref.7) | copy-start | bytes 1572868
  0.0 43.4 %copy-start = (bf16[2048,512]{1,0:T(8,128)(2,1)S(1)}, bf16[2048,512]{1,0:T(8,128)(2,1)}, u32[]{:S(2)}) copy-start(bf16[2048,512]{1,0:T(8,128)(2,1)} %wq_ref.7) | copy-start | bytes 6291460
  2.2 8.5 %collective-permute-start.1 = (bf16[256,512]{1,0:T(8,128)(2,1)S(1)}, bf16[256,512]{1,0:T(8,128)(2,1)S(1)}, u32[]{:S(2)}, u32[]{:S(2)}) collective-permute-start(bf16[256,512]{1,0:T(8,128)(2,1)S(1)} %get-tuple-element.23), channel_id=1, source_target_pairs={{12,0},{0,4},{4,8},{8,12},{13,1},{1,5},{5,9},{9,13},{14,2},{2,6},{... | collective-permute-start | bytes 786440 | tf_op jit(solution)/shard_map/ppermute | solution.py:114
  5.3 25.4 %collective-permute-start = (f32[256]{0:T(256)S(1)}, f32[256]{0:T(256)S(1)}, u32[]{:S(2)}, u32[]{:S(2)}) collective-permute-start(f32[256]{0:T(256)S(1)} %add_rsqrt_fusion), channel_id=1, source_target_pairs={{12,0},{0,4},{4,8},{8,12},{13,1},{1,5},{5,9},{9,13},{14,2},{2,6},{... | collective-permute-start | bytes 3080 | tf_op jit(solution)/shard_map/ppermute | solution.py:114
  6.6 20.7 %collective-permute-start.13 = (bf16[256,512]{1,0:T(8,128)(2,1)}, bf16[256,512]{1,0:T(8,128)(2,1)}, u32[]{:S(2)}, u32[]{:S(2)}) collective-permute-start(bf16[256,512]{1,0:T(8,128)(2,1)} %get-tuple-element.24), channel_id=1, source_target_pairs={{8,0},{12,4},{0,8},{4,12},{9,1},{13,5},{1,9},{5,13},{10,2},{14,6},... | collective-permute-start | bytes 786440 | tf_op jit(solution)/shard_map/ppermute | solution.py:114
  8.0 19.5 %collective-permute-start.7 = (bf16[256,512]{1,0:T(8,128)(2,1)}, bf16[256,512]{1,0:T(8,128)(2,1)S(1)}, u32[]{:S(2)}, u32[]{:S(2)}) collective-permute-start(bf16[256,512]{1,0:T(8,128)(2,1)} %get-tuple-element.25), channel_id=1, source_target_pairs={{4,0},{8,4},{12,8},{0,12},{5,1},{9,5},{13,9},{1,13},{6,2},{10,6},{... | collective-permute-start | bytes 786440 | tf_op jit(solution)/shard_map/ppermute | solution.py:114
  10.6 18.1 %collective-permute-start.3 = (bf16[256,512]{1,0:T(8,128)(2,1)S(1)}, bf16[256,512]{1,0:T(8,128)(2,1)S(1)}, u32[]{:S(2)}, u32[]{:S(2)}) collective-permute-start(bf16[256,512]{1,0:T(8,128)(2,1)S(1)} %collective-permute-done.1.refs_0_), channel_id=1, source_target_pairs={{2,0},{0,2},{3,1},{1,3},{6,4},{4,6},{7,5},{5,7},{10,8},{8,10},{11,... | collective-permute-start | bytes 786440 | tf_op jit(solution)/shard_map/ppermute | solution.py:114
  10.9 19.8 %collective-permute-start.2 = (bf16[256,512]{1,0:T(8,128)(2,1)S(1)}, bf16[256,512]{1,0:T(8,128)(2,1)S(1)}, u32[]{:S(2)}, u32[]{:S(2)}) collective-permute-start(bf16[256,512]{1,0:T(8,128)(2,1)S(1)} %collective-permute-done.1.refs_0_), channel_id=1, source_target_pairs={{1,0},{0,1},{3,2},{2,3},{5,4},{4,5},{7,6},{6,7},{9,8},{8,9},{11,10... | collective-permute-start | bytes 786440 | tf_op jit(solution)/shard_map/ppermute | solution.py:114
  27.2 7.7 %collective-permute-start.15 = (bf16[256,512]{1,0:T(8,128)(2,1)}, bf16[256,512]{1,0:T(8,128)(2,1)}, u32[]{:S(2)}, u32[]{:S(2)}) collective-permute-start(bf16[256,512]{1,0:T(8,128)(2,1)} %collective-permute-done.13.refs_0_), channel_id=1, source_target_pairs={{2,0},{0,2},{3,1},{1,3},{6,4},{4,6},{7,5},{5,7},{10,8},{8,10},{11,... | collective-permute-start | bytes 786440 | tf_op jit(solution)/shard_map/ppermute | solution.py:114
  27.5 13.0 %collective-permute-start.9 = (bf16[256,512]{1,0:T(8,128)(2,1)S(1)}, bf16[256,512]{1,0:T(8,128)(2,1)}, u32[]{:S(2)}, u32[]{:S(2)}) collective-permute-start(bf16[256,512]{1,0:T(8,128)(2,1)S(1)} %collective-permute-done.7.refs_0_), channel_id=1, source_target_pairs={{2,0},{0,2},{3,1},{1,3},{6,4},{4,6},{7,5},{5,7},{10,8},{8,10},{11,... | collective-permute-start | bytes 786440 | tf_op jit(solution)/shard_map/ppermute | solution.py:114
  28.8 14.5 %collective-permute-start.4 = (bf16[256,512]{1,0:T(8,128)(2,1)S(1)}, bf16[256,512]{1,0:T(8,128)(2,1)}, u32[]{:S(2)}, u32[]{:S(2)}) collective-permute-start(bf16[256,512]{1,0:T(8,128)(2,1)S(1)} %collective-permute-done.3.refs_2_), channel_id=1, source_target_pairs={{1,0},{0,1},{3,2},{2,3},{5,4},{4,5},{7,6},{6,7},{9,8},{8,9},{11,10... | collective-permute-start | bytes 786440 | tf_op jit(solution)/shard_map/ppermute | solution.py:114
  30.6 18.6 %collective-permute-start.14 = (bf16[256,512]{1,0:T(8,128)(2,1)}, bf16[256,512]{1,0:T(8,128)(2,1)}, u32[]{:S(2)}, u32[]{:S(2)}) collective-permute-start(bf16[256,512]{1,0:T(8,128)(2,1)} %collective-permute-done.13.refs_0_), channel_id=1, source_target_pairs={{1,0},{0,1},{3,2},{2,3},{5,4},{4,5},{7,6},{6,7},{9,8},{8,9},{11,10... | collective-permute-start | bytes 786440 | tf_op jit(solution)/shard_map/ppermute | solution.py:114
  31.4 25.7 %collective-permute-start.8 = (bf16[256,512]{1,0:T(8,128)(2,1)S(1)}, bf16[256,512]{1,0:T(8,128)(2,1)}, u32[]{:S(2)}, u32[]{:S(2)}) collective-permute-start(bf16[256,512]{1,0:T(8,128)(2,1)S(1)} %collective-permute-done.7.refs_0_), channel_id=1, source_target_pairs={{1,0},{0,1},{3,2},{2,3},{5,4},{4,5},{7,6},{6,7},{9,8},{8,9},{11,10... | collective-permute-start | bytes 786440 | tf_op jit(solution)/shard_map/ppermute | solution.py:114
  34.9 17.0 %collective-permute-start.16 = (bf16[256,512]{1,0:T(8,128)(2,1)}, bf16[256,512]{1,0:T(8,128)(2,1)}, u32[]{:S(2)}, u32[]{:S(2)}) collective-permute-start(bf16[256,512]{1,0:T(8,128)(2,1)} %collective-permute-done.15.refs_2_), channel_id=1, source_target_pairs={{1,0},{0,1},{3,2},{2,3},{5,4},{4,5},{7,6},{6,7},{9,8},{8,9},{11,10... | collective-permute-start | bytes 786440 | tf_op jit(solution)/shard_map/ppermute | solution.py:114
  40.5 16.5 %collective-permute-start.10 = (bf16[256,512]{1,0:T(8,128)(2,1)}, bf16[256,512]{1,0:T(8,128)(2,1)}, u32[]{:S(2)}, u32[]{:S(2)}) collective-permute-start(bf16[256,512]{1,0:T(8,128)(2,1)} %collective-permute-done.9.refs_2_), channel_id=1, source_target_pairs={{1,0},{0,1},{3,2},{2,3},{5,4},{4,5},{7,6},{6,7},{9,8},{8,9},{11,10... | collective-permute-start | bytes 786440 | tf_op jit(solution)/shard_map/ppermute | solution.py:114
  43.2 6.0 %collective-permute-start.12 = (f32[256]{0:T(256)S(1)}, f32[256]{0:T(256)S(1)}, u32[]{:S(2)}, u32[]{:S(2)}) collective-permute-start(f32[256]{0:T(256)S(1)} %add_rsqrt_fusion), channel_id=1, source_target_pairs={{8,0},{12,4},{0,8},{4,12},{9,1},{13,5},{1,9},{5,13},{10,2},{14,6},... | collective-permute-start | bytes 3080 | tf_op jit(solution)/shard_map/ppermute | solution.py:114
  48.6 13.7 %copy-start.14 = (f32[64]{0:T(128)S(1)}, f32[64]{0:T(128)}, u32[]{:S(2)}) copy-start(f32[64]{0:T(128)} %multiply_exponential_fusion) | copy-start | bytes 772
  49.3 7.7 %collective-permute-start.6 = (f32[256]{0:T(256)S(1)}, f32[256]{0:T(256)S(1)}, u32[]{:S(2)}, u32[]{:S(2)}) collective-permute-start(f32[256]{0:T(256)S(1)} %add_rsqrt_fusion), channel_id=1, source_target_pairs={{4,0},{8,4},{12,8},{0,12},{5,1},{9,5},{13,9},{1,13},{6,2},{10,6},{... | collective-permute-start | bytes 3080 | tf_op jit(solution)/shard_map/ppermute | solution.py:114
  49.3 19.0 %collective-permute-start.18 = (f16[256,128]{1,0:T(8,128)(2,1)}, f16[256,128]{1,0:T(8,128)(2,1)}, u32[]{:S(2)}, u32[]{:S(2)}) collective-permute-start(f16[256,128]{1,0:T(8,128)(2,1)} %convert_element_type.57), channel_id=1, source_target_pairs={{4,0},{8,4},{12,8},{0,12},{5,1},{9,5},{13,9},{1,13},{6,2},{10,6},{... | collective-permute-start | bytes 196616 | tf_op jit(solution)/shard_map/ppermute | solution.py:114
  56.1 13.8 %collective-permute-start.20 = (f16[256,128]{1,0:T(8,128)(2,1)}, f16[256,128]{1,0:T(8,128)(2,1)}, u32[]{:S(2)}, u32[]{:S(2)}) collective-permute-start(f16[256,128]{1,0:T(8,128)(2,1)} %convert_element_type.61), channel_id=1, source_target_pairs={{8,0},{12,4},{0,8},{4,12},{9,1},{13,5},{1,9},{5,13},{10,2},{14,6},... | collective-permute-start | bytes 196616 | tf_op jit(solution)/shard_map/ppermute | solution.py:114
  61.1 8.8 %collective-permute-start.19 = (f16[256,128]{1,0:T(8,128)(2,1)}, f16[256,128]{1,0:T(8,128)(2,1)}, u32[]{:S(2)}, u32[]{:S(2)}) collective-permute-start(f16[256,128]{1,0:T(8,128)(2,1)} %convert_element_type.59), channel_id=1, source_target_pairs={{12,0},{0,4},{4,8},{8,12},{13,1},{1,5},{5,9},{9,13},{14,2},{2,6},{... | collective-permute-start | bytes 196616 | tf_op jit(solution)/shard_map/ppermute | solution.py:114
  63.5 7.4 %copy-start.13 = (f32[256,64]{1,0:T(8,128)S(1)}, f32[256,64]{1,0:T(8,128)}, u32[]{:S(2)}) copy-start(f32[256,64]{1,0:T(8,128)} %get-tuple-element.31) | copy-start | bytes 196612
  63.6 10.2 %copy-start.16 = (s32[8]{0:T(128)S(1)}, s32[8]{0:T(128)}, u32[]{:S(2)}) copy-start(s32[8]{0:T(128)} %param.9) | copy-start | bytes 100
  64.9 1.8 %copy-start.4 = (f32[256,512]{1,0:T(8,128)S(1)}, f32[256,512]{1,0:T(8,128)}, u32[]{:S(2)}) copy-start(f32[256,512]{1,0:T(8,128)} %copy-done.3) | copy-start | bytes 1572868
  64.9 3.3 %copy-start.6 = (f32[256,512]{1,0:T(8,128)S(1)}, f32[256,512]{1,0:T(8,128)}, u32[]{:S(2)}) copy-start(f32[256,512]{1,0:T(8,128)} %copy-done.5) | copy-start | bytes 1572868
  66.4 31.3 %collective-permute-start.5 = (f16[256,512]{1,0:T(8,128)(2,1)S(1)}, f16[256,512]{1,0:T(8,128)(2,1)S(1)}, u32[]{:S(2)}, u32[]{:S(2)}) collective-permute-start(f16[256,512]{1,0:T(8,128)(2,1)S(1)} %convert_element_type.50), channel_id=1, source_target_pairs={{4,0},{8,4},{12,8},{0,12},{5,1},{9,5},{13,9},{1,13},{6,2},{10,6},{... | collective-permute-start | bytes 786440 | tf_op jit(solution)/shard_map/ppermute | solution.py:114
  66.7 30.9 %collective-permute-start.17 = (f16[256,512]{1,0:T(8,128)(2,1)S(1)}, f16[256,512]{1,0:T(8,128)(2,1)S(1)}, u32[]{:S(2)}, u32[]{:S(2)}) collective-permute-start(f16[256,512]{1,0:T(8,128)(2,1)S(1)} %convert_element_type.54), channel_id=1, source_target_pairs={{8,0},{12,4},{0,8},{4,12},{9,1},{13,5},{1,9},{5,13},{10,2},{14,6},... | collective-permute-start | bytes 786440 | tf_op jit(solution)/shard_map/ppermute | solution.py:114
  68.3 29.4 %collective-permute-start.11 = (f16[256,512]{1,0:T(8,128)(2,1)S(1)}, f16[256,512]{1,0:T(8,128)(2,1)S(1)}, u32[]{:S(2)}, u32[]{:S(2)}) collective-permute-start(f16[256,512]{1,0:T(8,128)(2,1)S(1)} %convert_element_type.52), channel_id=1, source_target_pairs={{12,0},{0,4},{4,8},{8,12},{13,1},{1,5},{5,9},{9,13},{14,2},{2,6},{... | collective-permute-start | bytes 786440 | tf_op jit(solution)/shard_map/ppermute | solution.py:114
  71.2 17.4 %collective-permute-start.22 = (bf16[256,128]{1,0:T(8,128)(2,1)S(1)}, bf16[256,128]{1,0:T(8,128)(2,1)S(1)}, u32[]{:S(2)}, u32[]{:S(2)}) collective-permute-start(bf16[256,128]{1,0:T(8,128)(2,1)S(1)} %get-tuple-element.21), channel_id=1, source_target_pairs={{0,4},{4,8},{8,12},{1,5},{5,9},{9,13},{2,6},{6,10},{10,14},{3,7},{... | collective-permute-start | bytes 196616 | tf_op jit(solution)/shard_map/ppermute | solution.py:231
  72.5 24.0 %collective-permute-start.21 = (bf16[256,128]{1,0:T(8,128)(2,1)S(1)}, bf16[256,128]{1,0:T(8,128)(2,1)S(1)}, u32[]{:S(2)}, u32[]{:S(2)}) collective-permute-start(bf16[256,128]{1,0:T(8,128)(2,1)S(1)} %get-tuple-element.21), channel_id=1, source_target_pairs={{0,8},{4,12},{1,9},{5,13},{2,10},{6,14},{3,11},{7,15},{16,24},{20,... | collective-permute-start | bytes 196616 | tf_op jit(solution)/shard_map/ppermute | solution.py:231
  96.5 2.2 %collective-permute-start.23 = (bf16[768,128]{1,0:T(8,128)(2,1)S(1)}, bf16[768,128]{1,0:T(8,128)(2,1)S(1)}, u32[]{:S(2)}, u32[]{:S(2)}) collective-permute-start(bf16[768,128]{1,0:T(8,128)(2,1)S(1)} %pad_maximum_fusion.half_ref), channel_id=1, source_target_pairs={{1,0},{0,1},{3,2},{2,3},{5,4},{4,5},{7,6},{6,7},{9,8},{8,9},{11,10... | collective-permute-start | bytes 589832 | tf_op jit(solution)/shard_map/ppermute | solution.py:114
  (9 other events, 7.8 us)

commit v2 on v1

--- a/solution.py
+++ b/solution.py
@@ -118,54 +118,44 @@
     return jnp.dot(a, b, preferred_element_type=jnp.float32)
 
 
-def project_kernel(scale, count, places, factor_ref, gain_ref, wq_ref, wkv_ref, *refs):
-    pieces, (q_ref, kv_ref, block) = refs[:count], refs[count:]
+def assemble_kernel(count, places, factor_ref, gain_ref, *refs):
+    pieces, block_ref = refs[:count], refs[count]
+    rows = block_ref.shape[0]
+    square = (rows, rows)
+    same = lax.broadcasted_iota(jnp.int32, square, 0) == lax.broadcasted_iota(jnp.int32, square, 1)
+    factor = jnp.sum(jnp.where(same, factor_ref[...], 0.0), axis=1, keepdims=True)
+    factor = jnp.broadcast_to(factor, (rows, 128))
     for i, piece in enumerate(pieces):
         for j in range(0, piece.shape[1], 128):
             chosen = pl.ds(pl.multiple_of(places[i] + j, 128), 128)
             part = piece[:, j : j + 128].astype(jnp.float32)
-            normed = part * factor_ref[...] * gain_ref[:, chosen]
-            block[:, chosen] = normed.astype(jnp.bfloat16)
-    kv_ref[...] = dot(block[...], wkv_ref[...]) * scale
-    q_ref[...] = dot(block[...], wq_ref[...]) * scale
-
-
-def project(pieces, places, factor, gain, w_query, w_keyval, scale):
-    rows, depth = pieces[0].shape[0], w_query.shape[0]
+            block_ref[:, chosen] = (part * factor * gain_ref[:, chosen]).astype(jnp.bfloat16)
+
+
+def assemble(pieces, places, factor, gain):
+    rows, depth = pieces[0].shape[0], gain.shape[0]
     widths = [piece.shape[1] for piece in pieces]
-    columns = w_query.shape[1], w_keyval.shape[1]
     if any(w % 128 for w in widths):
         block = jnp.zeros((rows, depth), jnp.bfloat16)
         for piece, place in zip(pieces, places):
             block = lax.dynamic_update_slice_in_dim(block, piece, place, 1)
-        block = (block.astype(jnp.float32) * factor[:, None] * gain[None, :]).astype(jnp.bfloat16)
-        return dot(block, w_query) * scale, dot(block, w_keyval) * scale
+        return (block.astype(jnp.float32) * factor[:, None] * gain[None, :]).astype(jnp.bfloat16)
     in_vmem = pl.BlockSpec(memory_space=pltpu.VMEM)
     return pl.pallas_call(
-        functools.partial(project_kernel, scale, len(pieces)),
-        out_shape=[jax.ShapeDtypeStruct((rows, w), jnp.float32) for w in columns],
-        in_specs=[pl.BlockSpec(memory_space=pltpu.SMEM)] + [in_vmem] * (4 + len(pieces)),
-        out_specs=[in_vmem, in_vmem],
-        scratch_shapes=[pltpu.VMEM((rows, depth), jnp.bfloat16)],
+        functools.partial(assemble_kernel, len(pieces)),
+        out_shape=jax.ShapeDtypeStruct((rows, depth), jnp.bfloat16),
+        in_specs=[pl.BlockSpec(memory_space=pltpu.SMEM)] + [in_vmem] * (2 + len(pieces)),
+        out_specs=in_vmem,
         cost_estimate=pl.CostEstimate(
-            flops=2 * rows * depth * sum(columns),
-            bytes_accessed=2 * depth * sum(columns) + 2 * rows * depth,
-            transcendentals=0,
+            flops=4 * rows * depth, bytes_accessed=4 * rows * depth, transcendentals=0
         ),
         compiler_params=pltpu.CompilerParams(vmem_limit_bytes=KERNEL_VMEM),
-        name="project",
-    )(
-        jnp.stack(places).astype(jnp.int32),
-        jnp.broadcast_to(factor[:, None], (rows, 128)),
-        gain[None, :],
-        w_query,
-        w_keyval,
-        *pieces,
-    )
-
-
-def offsets_of(n):
-    return sorted(range(1, n), key=lambda d: (min(d, n - d), d))
+        name="assemble",
+    )(jnp.stack(places).astype(jnp.int32), factor[None, :], gain[None, :], *pieces)
+
+
+def groups_of(n):
+    return [sorted({d, n - d}) for d in range(n // 2, 0, -1)]
 
 
 def shards(sizes, hidden_states, norm_gain, w_query, w_keyval, doc_lengths):
@@ -175,7 +165,7 @@
     depth = w_query.shape[0]
     piece = depth // quarters
     s, m, c = lax.axis_index("seq"), lax.axis_index("mp"), lax.axis_index("sub")
-    offsets = offsets_of(n)
+    offsets = [d for group in groups_of(n) for d in group]
 
     bound = GAIN_BOUND * math.sqrt(width) * W_BOUND * math.sqrt(depth)
     wire_scale = 2.0 ** min(0, math.floor(math.log2(WIRE_MAX / bound)))
@@ -197,9 +187,8 @@
     scalars = jnp.concatenate([jnp.stack([s, c]).astype(jnp.int32), doc_lengths])
 
     own = lax.dynamic_slice_in_dim(hidden_states, s * depth, depth, 1)
-    query_sum, keyval_sum = project(
-        [own], [jnp.zeros((), jnp.int32)], factor, gain, w_query, w_keyval, 1.0
-    )
+    own = assemble([own], [jnp.zeros((), jnp.int32)], factor, gain)
+    keyval_sum, query_sum = dot(own, w_keyval), dot(own, w_query)
     places = [
         (lax.rem(m + i, m_size) * c_size + lax.rem(c + j, c_size)) * piece
         for i in range(m_size)
@@ -212,9 +201,11 @@
             near = pull(arrived[d], "mp", i, m_size) if i else arrived[d]
             pieces += [near]
             pieces += [pull(near, "sub", j, c_size) for j in range(1, c_size)]
-        q_part, kv_part = project(pieces, places, factors[d], gain, w_query, w_keyval, wire_scale)
-        kv_parts.append(pull(kv_part.astype(jnp.float16), "seq", d, n))
-        q_parts.append(pull(q_part.astype(jnp.float16), "seq", d, n))
+        block = assemble(pieces, places, factors[d], gain)
+        kv_part = (dot(block, w_keyval) * wire_scale).astype(jnp.float16)
+        q_part = (dot(block, w_query) * wire_scale).astype(jnp.float16)
+        kv_parts.append(pull(kv_part, "seq", d, n))
+        q_parts.append(pull(q_part, "seq", d, n))
     for part in kv_parts:
         keyval_sum = keyval_sum + part.astype(jnp.float32) * unscale
     for part in q_parts:

time: 102 us -> 93 us (0.912)
  the two profiles are of different devices: /device:TPU:31 before, /device:TPU:29 now
where the time goes in v2:
time: 93 us; the launch traced here: 92.6 us
  waiting for transfers between devices  41.2 us (44%)
  starting transfers between devices  26.1 us (28%)
  Pallas kernels  7.72 us (8%)
  other arithmetic  6.48 us (7%)
  matrix products  6.36 us (7%)
  local copies, waits for them, and re-layouts  4.48 us (5%)
    ppermute x22, starting transfers between devices, pull(): return lax.ppermute(array, axis, pairs)  23.5 us
    ppermute x2, waiting for transfers between devices, shards(): lax.ppermute(own_half, 'seq', [(i, i + e) for i in range(n - e)])  23.5 us
    ppermute x22, waiting for transfers between devices, pull(): return lax.ppermute(array, axis, pairs)  17.7 us
    dot_general x8, matrix products, dot(): return jnp.dot(a, b, preferred_element_type=jnp.float32)  6.36 us
    pallas_call x4, Pallas kernels, assemble(): pl.pallas_call(functools.partial(assemble_kernel, len(pieces)), out_shape...  4.6 us
    reduce_sum x1, other arithmetic, inverse_norm(): return lax.rsqrt(jnp.mean(as_float * as_float, axis=-1) + 1e-05)  3.26 us
    pallas_call x1, Pallas kernels, attend(): pl.pallas_call(functools.partial(attend_kernel, reach, chunk, docs), out_...  3.12 us
    ppermute x2, starting transfers between devices, shards(): lax.ppermute(own_half, 'seq', [(i, i + e) for i in range(n - e)])  2.58 us
  transfers between devices with their start and end apart: 24, of which 6 were waited for; matrix products, arithmetic and copies ran while one was open for 15% of the time, Pallas kernels for 5%

profile of v2, /device:TPU:29, one launch (start us, length us, event | category | flops | bytes accessed | tf_op | source)
XLA Modules:
  0.0 92.6 jit_solution(5152699452122017463)
XLA Ops:
  0.0 3.3 %multiply_reduce_fusion = f32[256]{0:T(256)S(1)} fusion(bf16[256,8192]{1,0:T(8,128)(2,1)} %param.5), kind=kLoop, calls=%fused_computation | loop fusion | flops 6291200 | bytes 4195328 | tf_op jit(solution)/shard_map/reduce_sum | solution.py:24
  3.4 2.0 %constant_dynamic-slice_fusion.2 = (bf16[256,512]{1,0:T(8,128)(2,1)}, bf16[256,512]{1,0:T(8,128)(2,1)}, bf16[256,512]{1,0:T(8,128)(2,1)}) fusion(bf16[256,8192]{1,0:T(8,128)(2,1)} %param.5, s32[]{:T(128)S(6)} %select_n.26, s32[]{:T(128)S(6)} %select_n.28, s32[]{:T(128)S(6)} %select_n.27), kind=kLoop, calls=%fused_computation.30 | loop fusion | bytes 1572876 | tf_op jit(solution)/shard_map/dynamic_slice | solution.py:178
  5.4 2.3 %collective-permute-start.1 = (bf16[256,512]{1,0:T(8,128)(2,1)}, bf16[256,512]{1,0:T(8,128)(2,1)}, u32[]{:S(2)}, u32[]{:S(2)}) collective-permute-start(bf16[256,512]{1,0:T(8,128)(2,1)} %get-tuple-element.7), channel_id=1, source_target_pairs={{8,0},{12,4},{0,8},{4,12},{9,1},{13,5},{1,9},{5,13},{10,2},{14,6},... | collective-permute-start | bytes 786440 | tf_op jit(solution)/shard_map/ppermute | solution.py:114
  7.9 3.1 %collective-permute-start.7 = (bf16[256,512]{1,0:T(8,128)(2,1)}, bf16[256,512]{1,0:T(8,128)(2,1)S(1)}, u32[]{:S(2)}, u32[]{:S(2)}) collective-permute-start(bf16[256,512]{1,0:T(8,128)(2,1)} %get-tuple-element.9), channel_id=1, source_target_pairs={{12,0},{0,4},{4,8},{8,12},{13,1},{1,5},{5,9},{9,13},{14,2},{2,6},{... | collective-permute-start | bytes 786440 | tf_op jit(solution)/shard_map/ppermute | solution.py:114
  11.2 1.3 %constant_dynamic-slice_fusion.3.refs_0_ = bf16[256,2048]{1,0:T(8,128)(2,1)S(1)} fusion(bf16[256,8192]{1,0:T(8,128)(2,1)} %param.5, s32[]{:T(128)S(6)} %select_n.25), kind=kLoop, calls=%fused_computation.31 | loop fusion | bytes 2097156 | tf_op jit(solution)/shard_map/dynamic_slice | solution.py:189
  13.8 1.5 %fusion.11 = f32[256,512]{1,0:T(8,128)} fusion(bf16[256,2048]{1,0:T(8,128)(2,1)S(1)} %assemble.4, bf16[2048,512]{1,0:T(8,128)(2,1)S(1)} %copy-done), kind=kOutput, calls=%fused_computation.38 | convolution fusion | flops 536870912 | bytes 3670016 | tf_op jit(solution)/shard_map/dot_general | solution.py:118
  15.9 10.1 %collective-permute-done.1.refs_0_ = bf16[256,512]{1,0:T(8,128)(2,1)} collective-permute-done((bf16[256,512]{1,0:T(8,128)(2,1)}, bf16[256,512]{1,0:T(8,128)(2,1)}, u32[]{:S(2)}, u32[]{:S(2)}) %collective-permute-start.1) | collective-permute-done | bytes 262176 | tf_op jit(solution)/shard_map/ppermute | solution.py:114
  26.0 1.2 %collective-permute-start.3 = (bf16[256,512]{1,0:T(8,128)(2,1)}, bf16[256,512]{1,0:T(8,128)(2,1)}, u32[]{:S(2)}, u32[]{:S(2)}) collective-permute-start(bf16[256,512]{1,0:T(8,128)(2,1)} %collective-permute-done.1.refs_0_), channel_id=1, source_target_pairs={{2,0},{0,2},{3,1},{1,3},{6,4},{4,6},{7,5},{5,7},{10,8},{8,10},{11,... | collective-permute-start | bytes 786440 | tf_op jit(solution)/shard_map/ppermute | solution.py:114
  27.2 1.5 %fusion.12 = f32[256,128]{1,0:T(8,128)S(1)} fusion(bf16[256,2048]{1,0:T(8,128)(2,1)S(1)} %assemble.4, bf16[2048,128]{1,0:T(8,128)(2,1)} %param.8), kind=kOutput, calls=%fused_computation.39 | convolution fusion | flops 134217728 | bytes 1703936 | tf_op jit(solution)/shard_map/dot_general | solution.py:118
  28.7 0.9 %collective-permute-start.2 = (bf16[256,512]{1,0:T(8,128)(2,1)}, bf16[256,512]{1,0:T(8,128)(2,1)S(1)}, u32[]{:S(2)}, u32[]{:S(2)}) collective-permute-start(bf16[256,512]{1,0:T(8,128)(2,1)} %collective-permute-done.1.refs_0_), channel_id=1, source_target_pairs={{1,0},{0,1},{3,2},{2,3},{5,4},{4,5},{7,6},{6,7},{9,8},{8,9},{11,10... | collective-permute-start | bytes 786440 | tf_op jit(solution)/shard_map/ppermute | solution.py:114
  29.9 3.7 %collective-permute-done.3.refs_2_ = bf16[256,512]{1,0:T(8,128)(2,1)} collective-permute-done((bf16[256,512]{1,0:T(8,128)(2,1)}, bf16[256,512]{1,0:T(8,128)(2,1)}, u32[]{:S(2)}, u32[]{:S(2)}) %collective-permute-start.3) | collective-permute-done | bytes 262176 | tf_op jit(solution)/shard_map/ppermute | solution.py:114
  33.6 2.5 %collective-permute-start.4 = (bf16[256,512]{1,0:T(8,128)(2,1)}, bf16[256,512]{1,0:T(8,128)(2,1)S(1)}, u32[]{:S(2)}, u32[]{:S(2)}) collective-permute-start(bf16[256,512]{1,0:T(8,128)(2,1)} %collective-permute-done.3.refs_2_), channel_id=1, source_target_pairs={{1,0},{0,1},{3,2},{2,3},{5,4},{4,5},{7,6},{6,7},{9,8},{8,9},{11,10... | collective-permute-start | bytes 786440 | tf_op jit(solution)/shard_map/ppermute | solution.py:114
  36.1 1.8 %fusion.9 = (f32[256,64]{1,0:T(8,128)S(1)}, f32[256,64]{1,0:T(8,128)}, f32[256,64]{1,0:T(8,128)}) fusion(f32[64]{0:T(128)} %multiply_exponential_fusion, f32[256]{0:T(256)S(1)} %subtract_convert_fusion), kind=kLoop, calls=%fused_computation.24 | loop fusion | flops 32768 | bytes 197888 | tf_op jit(solution)/shard_map/neg | solution.py:43
  38.1 3.2 %collective-permute-start.6 = (f32[256]{0:T(256)S(1)}, f32[256]{0:T(256)S(1)}, u32[]{:S(2)}, u32[]{:S(2)}) collective-permute-start(f32[256]{0:T(256)S(1)} %add_rsqrt_fusion), channel_id=1, source_target_pairs={{12,0},{0,4},{4,8},{8,12},{13,1},{1,5},{5,9},{9,13},{14,2},{2,6},{... | collective-permute-start | bytes 3080 | tf_op jit(solution)/shard_map/ppermute | solution.py:114
  41.9 1.2 %collective-permute-start.9 = (bf16[256,512]{1,0:T(8,128)(2,1)S(1)}, bf16[256,512]{1,0:T(8,128)(2,1)S(1)}, u32[]{:S(2)}, u32[]{:S(2)}) collective-permute-start(bf16[256,512]{1,0:T(8,128)(2,1)S(1)} %collective-permute-done.7.refs_0_), channel_id=1, source_target_pairs={{2,0},{0,2},{3,1},{1,3},{6,4},{4,6},{7,5},{5,7},{10,8},{8,10},{11,... | collective-permute-start | bytes 786440 | tf_op jit(solution)/shard_map/ppermute | solution.py:114
  43.4 1.6 %assemble.5 = bf16[256,2048]{1,0:T(8,128)(2,1)S(1)} custom-call(s32[4]{0:T(128)S(1)} %pad_add_fusion.1.places, f32[1,256]{1,0:T(1,128)S(1)} %bitcast.35, f32[1,2048]{1,0:T(1,128)S(1)} %bitcast.31, bf16[256,512]{1,0:T(8,128)(2,1)} %collective-permute-done.1.refs_0_, bf16[256,512]{1,0:T(8,128)(2,1)S(1)} %collective-permute-done.2.refs_1_, ...), custom_call_target="tpu_custom_call" | custom-call | flops 2097152 | bytes 2097152 | tf_op jit(solution)/shard_map/assemble/pallas_call | solution.py:144
  45.0 0.7 fusion
  46.7 3.0 %collective-permute-done.9.refs_2_ = bf16[256,512]{1,0:T(8,128)(2,1)S(1)} collective-permute-done((bf16[256,512]{1,0:T(8,128)(2,1)S(1)}, bf16[256,512]{1,0:T(8,128)(2,1)S(1)}, u32[]{:S(2)}, u32[]{:S(2)}) %collective-permute-start.9) | collective-permute-done | bytes 262176 | tf_op jit(solution)/shard_map/ppermute | solution.py:114
  49.7 0.9 %collective-permute-start.10 = (bf16[256,512]{1,0:T(8,128)(2,1)S(1)}, bf16[256,512]{1,0:T(8,128)(2,1)S(1)}, u32[]{:S(2)}, u32[]{:S(2)}) collective-permute-start(bf16[256,512]{1,0:T(8,128)(2,1)S(1)} %collective-permute-done.9.refs_2_), channel_id=1, source_target_pairs={{1,0},{0,1},{3,2},{2,3},{5,4},{4,5},{7,6},{6,7},{9,8},{8,9},{11,10... | collective-permute-start | bytes 786440 | tf_op jit(solution)/shard_map/ppermute | solution.py:114
  50.6 1.5 %assemble.7 = bf16[256,2048]{1,0:T(8,128)(2,1)S(1)} custom-call(s32[4]{0:T(128)S(1)} %pad_add_fusion.1.places, f32[1,256]{1,0:T(1,128)S(1)} %bitcast.37, f32[1,2048]{1,0:T(1,128)S(1)} %bitcast.32, bf16[256,512]{1,0:T(8,128)(2,1)} %collective-permute-done.13.refs_0_, bf16[256,512]{1,0:T(8,128)(2,1)S(1)} %collective-permute-done.14.refs_1_, ...), custom_call_target="tpu_custom_call" | custom-call | flops 2097152 | bytes 2097152 | tf_op jit(solution)/shard_map/assemble/pallas_call | solution.py:144
  52.1 0.7 fusion.2
  53.4 1.1 %assemble.6 = bf16[256,2048]{1,0:T(8,128)(2,1)S(1)} custom-call(s32[4]{0:T(128)S(1)} %pad_add_fusion.1.places, f32[1,256]{1,0:T(1,128)S(1)} %bitcast.36, f32[1,2048]{1,0:T(1,128)S(1)} %bitcast.33, bf16[256,512]{1,0:T(8,128)(2,1)S(1)} %collective-permute-done.7.refs_0_, bf16[256,512]{1,0:T(8,128)(2,1)S(1)} %collective-permute-done.8.refs_1_, ...), custom_call_target="tpu_custom_call" | custom-call | flops 2097152 | bytes 2097152 | tf_op jit(solution)/shard_map/assemble/pallas_call | solution.py:144
  54.9 1.5 %collective-permute-start.19 = (f16[256,128]{1,0:T(8,128)(2,1)S(1)}, f16[256,128]{1,0:T(8,128)(2,1)S(1)}, u32[]{:S(2)}, u32[]{:S(2)}) collective-permute-start(f16[256,128]{1,0:T(8,128)(2,1)S(1)} %fusion.4), channel_id=1, source_target_pairs={{4,0},{8,4},{12,8},{0,12},{5,1},{9,5},{13,9},{1,13},{6,2},{10,6},{... | collective-permute-start | bytes 196616 | tf_op jit(solution)/shard_map/ppermute | solution.py:114
  57.1 2.4 %collective-permute-start.5 = (f16[256,512]{1,0:T(8,128)(2,1)S(1)}, f16[256,512]{1,0:T(8,128)(2,1)S(1)}, u32[]{:S(2)}, u32[]{:S(2)}) collective-permute-start(f16[256,512]{1,0:T(8,128)(2,1)S(1)} %fusion), channel_id=1, source_target_pairs={{8,0},{12,4},{0,8},{4,12},{9,1},{13,5},{1,9},{5,13},{10,2},{14,6},... | collective-permute-start | bytes 786440 | tf_op jit(solution)/shard_map/ppermute | solution.py:114
  59.5 0.9 collective-permute-start.17
  61.3 1.3 %collective-permute-start.22 = (bf16[256,128]{1,0:T(8,128)(2,1)S(1)}, bf16[256,128]{1,0:T(8,128)(2,1)S(1)}, u32[]{:S(2)}, u32[]{:S(2)}) collective-permute-start(bf16[256,128]{1,0:T(8,128)(2,1)S(1)} %get-tuple-element.5), channel_id=1, source_target_pairs={{0,4},{4,8},{8,12},{1,5},{5,9},{9,13},{2,6},{6,10},{10,14},{3,7},{... | collective-permute-start | bytes 196616 | tf_op jit(solution)/shard_map/ppermute | solution.py:222
  62.6 1.3 %collective-permute-start.21 = (bf16[256,128]{1,0:T(8,128)(2,1)S(1)}, bf16[256,128]{1,0:T(8,128)(2,1)S(1)}, u32[]{:S(2)}, u32[]{:S(2)}) collective-permute-start(bf16[256,128]{1,0:T(8,128)(2,1)S(1)} %get-tuple-element.5), channel_id=1, source_target_pairs={{0,8},{4,12},{1,9},{5,13},{2,10},{6,14},{3,11},{7,15},{16,24},{20,... | collective-permute-start | bytes 196616 | tf_op jit(solution)/shard_map/ppermute | solution.py:222
  64.0 9.4 %collective-permute-done.22 = bf16[256,128]{1,0:T(8,128)(2,1)S(1)} collective-permute-done((bf16[256,128]{1,0:T(8,128)(2,1)S(1)}, bf16[256,128]{1,0:T(8,128)(2,1)S(1)}, u32[]{:S(2)}, u32[]{:S(2)}) %collective-permute-start.22) | collective-permute-done | bytes 65568 | tf_op jit(solution)/shard_map/ppermute | solution.py:222
  73.4 14.0 %collective-permute-done.21 = bf16[256,128]{1,0:T(8,128)(2,1)S(1)} collective-permute-done((bf16[256,128]{1,0:T(8,128)(2,1)S(1)}, bf16[256,128]{1,0:T(8,128)(2,1)S(1)}, u32[]{:S(2)}, u32[]{:S(2)}) %collective-permute-start.21) | collective-permute-done | bytes 65568 | tf_op jit(solution)/shard_map/ppermute | solution.py:222
  87.5 0.9 collective-permute-start.23
  88.6 0.9 collective-permute-done.23.other_ref
  89.5 3.1 %attend.1 = bf16[256,512]{1,0:T(8,128)(2,1)} custom-call(s32[10]{0:T(128)S(1)} %pad_add_fusion.scalars, f32[256,512]{1,0:T(8,128)S(1)} %multiply_add_fusion.query_ref, f32[256,128]{1,0:T(8,128)S(1)} %get-tuple-element.10.cos_ref, f32[256,128]{1,0:T(8,128)S(1)} %get-tuple-element.6.sin_ref, bf16[768,128]{1,0:T(8,128)(2,1)S(1)} %pad_maximum_fusion.half_ref, ...), custom_call_target="tpu_custom_call" | custom-call | flops 402653184 | bytes 1441792 | tf_op jit(solution)/shard_map/attend/pallas_call | solution.py:96
  (62 shorter events, 7.4 us)
Async XLA Ops:
  0.0 13.8 %copy-start = (bf16[2048,512]{1,0:T(8,128)(2,1)S(1)}, bf16[2048,512]{1,0:T(8,128)(2,1)}, u32[]{:S(2)}) copy-start(bf16[2048,512]{1,0:T(8,128)(2,1)} %param.7) | copy-start | bytes 6291460
  0.0 11.0 %copy-start.5 = (s32[8]{0:T(128)S(1)}, s32[8]{0:T(128)}, u32[]{:S(2)}) copy-start(s32[8]{0:T(128)} %param.9) | copy-start | bytes 100
  3.3 34.7 %collective-permute-start = (f32[256]{0:T(256)S(1)}, f32[256]{0:T(256)S(1)}, u32[]{:S(2)}, u32[]{:S(2)}) collective-permute-start(f32[256]{0:T(256)S(1)} %add_rsqrt_fusion), channel_id=1, source_target_pairs={{8,0},{12,4},{0,8},{4,12},{9,1},{13,5},{1,9},{5,13},{10,2},{14,6},... | collective-permute-start | bytes 3080 | tf_op jit(solution)/shard_map/ppermute | solution.py:114
  5.4 20.6 %collective-permute-start.1 = (bf16[256,512]{1,0:T(8,128)(2,1)}, bf16[256,512]{1,0:T(8,128)(2,1)}, u32[]{:S(2)}, u32[]{:S(2)}) collective-permute-start(bf16[256,512]{1,0:T(8,128)(2,1)} %get-tuple-element.7), channel_id=1, source_target_pairs={{8,0},{12,4},{0,8},{4,12},{9,1},{13,5},{1,9},{5,13},{10,2},{14,6},... | collective-permute-start | bytes 786440 | tf_op jit(solution)/shard_map/ppermute | solution.py:114
  7.7 21.9 %collective-permute-start.13 = (bf16[256,512]{1,0:T(8,128)(2,1)}, bf16[256,512]{1,0:T(8,128)(2,1)}, u32[]{:S(2)}, u32[]{:S(2)}) collective-permute-start(bf16[256,512]{1,0:T(8,128)(2,1)} %get-tuple-element.8), channel_id=1, source_target_pairs={{4,0},{8,4},{12,8},{0,12},{5,1},{9,5},{13,9},{1,13},{6,2},{10,6},{... | collective-permute-start | bytes 786440 | tf_op jit(solution)/shard_map/ppermute | solution.py:114
  7.9 30.2 %collective-permute-start.7 = (bf16[256,512]{1,0:T(8,128)(2,1)}, bf16[256,512]{1,0:T(8,128)(2,1)S(1)}, u32[]{:S(2)}, u32[]{:S(2)}) collective-permute-start(bf16[256,512]{1,0:T(8,128)(2,1)} %get-tuple-element.9), channel_id=1, source_target_pairs={{12,0},{0,4},{4,8},{8,12},{13,1},{1,5},{5,9},{9,13},{14,2},{2,6},{... | collective-permute-start | bytes 786440 | tf_op jit(solution)/shard_map/ppermute | solution.py:114
  26.0 7.6 %collective-permute-start.3 = (bf16[256,512]{1,0:T(8,128)(2,1)}, bf16[256,512]{1,0:T(8,128)(2,1)}, u32[]{:S(2)}, u32[]{:S(2)}) collective-permute-start(bf16[256,512]{1,0:T(8,128)(2,1)} %collective-permute-done.1.refs_0_), channel_id=1, source_target_pairs={{2,0},{0,2},{3,1},{1,3},{6,4},{4,6},{7,5},{5,7},{10,8},{8,10},{11,... | collective-permute-start | bytes 786440 | tf_op jit(solution)/shard_map/ppermute | solution.py:114
  28.7 12.6 %collective-permute-start.2 = (bf16[256,512]{1,0:T(8,128)(2,1)}, bf16[256,512]{1,0:T(8,128)(2,1)S(1)}, u32[]{:S(2)}, u32[]{:S(2)}) collective-permute-start(bf16[256,512]{1,0:T(8,128)(2,1)} %collective-permute-done.1.refs_0_), channel_id=1, source_target_pairs={{1,0},{0,1},{3,2},{2,3},{5,4},{4,5},{7,6},{6,7},{9,8},{8,9},{11,10... | collective-permute-start | bytes 786440 | tf_op jit(solution)/shard_map/ppermute | solution.py:114
  29.6 12.2 %collective-permute-start.15 = (bf16[256,512]{1,0:T(8,128)(2,1)}, bf16[256,512]{1,0:T(8,128)(2,1)S(1)}, u32[]{:S(2)}, u32[]{:S(2)}) collective-permute-start(bf16[256,512]{1,0:T(8,128)(2,1)} %collective-permute-done.13.refs_0_), channel_id=1, source_target_pairs={{2,0},{0,2},{3,1},{1,3},{6,4},{4,6},{7,5},{5,7},{10,8},{8,10},{11,... | collective-permute-start | bytes 786440 | tf_op jit(solution)/shard_map/ppermute | solution.py:114
  33.6 9.5 %collective-permute-start.4 = (bf16[256,512]{1,0:T(8,128)(2,1)}, bf16[256,512]{1,0:T(8,128)(2,1)S(1)}, u32[]{:S(2)}, u32[]{:S(2)}) collective-permute-start(bf16[256,512]{1,0:T(8,128)(2,1)} %collective-permute-done.3.refs_2_), channel_id=1, source_target_pairs={{1,0},{0,1},{3,2},{2,3},{5,4},{4,5},{7,6},{6,7},{9,8},{8,9},{11,10... | collective-permute-start | bytes 786440 | tf_op jit(solution)/shard_map/ppermute | solution.py:114
  38.0 8.4 %collective-permute-start.12 = (f32[256]{0:T(256)S(1)}, f32[256]{0:T(256)S(1)}, u32[]{:S(2)}, u32[]{:S(2)}) collective-permute-start(f32[256]{0:T(256)S(1)} %add_rsqrt_fusion), channel_id=1, source_target_pairs={{4,0},{8,4},{12,8},{0,12},{5,1},{9,5},{13,9},{1,13},{6,2},{10,6},{... | collective-permute-start | bytes 3080 | tf_op jit(solution)/shard_map/ppermute | solution.py:114
  38.1 15.3 %collective-permute-start.6 = (f32[256]{0:T(256)S(1)}, f32[256]{0:T(256)S(1)}, u32[]{:S(2)}, u32[]{:S(2)}) collective-permute-start(f32[256]{0:T(256)S(1)} %add_rsqrt_fusion), channel_id=1, source_target_pairs={{12,0},{0,4},{4,8},{8,12},{13,1},{1,5},{5,9},{9,13},{14,2},{2,6},{... | collective-permute-start | bytes 3080 | tf_op jit(solution)/shard_map/ppermute | solution.py:114
  41.3 9.3 %collective-permute-start.14 = (bf16[256,512]{1,0:T(8,128)(2,1)}, bf16[256,512]{1,0:T(8,128)(2,1)S(1)}, u32[]{:S(2)}, u32[]{:S(2)}) collective-permute-start(bf16[256,512]{1,0:T(8,128)(2,1)} %collective-permute-done.13.refs_0_), channel_id=1, source_target_pairs={{1,0},{0,1},{3,2},{2,3},{5,4},{4,5},{7,6},{6,7},{9,8},{8,9},{11,10... | collective-permute-start | bytes 786440 | tf_op jit(solution)/shard_map/ppermute | solution.py:114
  41.9 7.8 %collective-permute-start.9 = (bf16[256,512]{1,0:T(8,128)(2,1)S(1)}, bf16[256,512]{1,0:T(8,128)(2,1)S(1)}, u32[]{:S(2)}, u32[]{:S(2)}) collective-permute-start(bf16[256,512]{1,0:T(8,128)(2,1)S(1)} %collective-permute-done.7.refs_0_), channel_id=1, source_target_pairs={{2,0},{0,2},{3,1},{1,3},{6,4},{4,6},{7,5},{5,7},{10,8},{8,10},{11,... | collective-permute-start | bytes 786440 | tf_op jit(solution)/shard_map/ppermute | solution.py:114
  43.1 7.5 %collective-permute-start.16 = (bf16[256,512]{1,0:T(8,128)(2,1)S(1)}, bf16[256,512]{1,0:T(8,128)(2,1)S(1)}, u32[]{:S(2)}, u32[]{:S(2)}) collective-permute-start(bf16[256,512]{1,0:T(8,128)(2,1)S(1)} %collective-permute-done.15.refs_2_), channel_id=1, source_target_pairs={{1,0},{0,1},{3,2},{2,3},{5,4},{4,5},{7,6},{6,7},{9,8},{8,9},{11,10... | collective-permute-start | bytes 786440 | tf_op jit(solution)/shard_map/ppermute | solution.py:114
  45.0 1.0 %copy-start.1 = (bf16[2048,128]{1,0:T(8,128)(2,1)S(1)}, bf16[2048,128]{1,0:T(8,128)(2,1)}, u32[]{:S(2)}) copy-start(bf16[2048,128]{1,0:T(8,128)(2,1)} %param.8) | copy-start | bytes 1572868
  46.5 6.9 %collective-permute-start.8 = (bf16[256,512]{1,0:T(8,128)(2,1)S(1)}, bf16[256,512]{1,0:T(8,128)(2,1)S(1)}, u32[]{:S(2)}, u32[]{:S(2)}) collective-permute-start(bf16[256,512]{1,0:T(8,128)(2,1)S(1)} %collective-permute-done.7.refs_0_), channel_id=1, source_target_pairs={{1,0},{0,1},{3,2},{2,3},{5,4},{4,5},{7,6},{6,7},{9,8},{8,9},{11,10... | collective-permute-start | bytes 786440 | tf_op jit(solution)/shard_map/ppermute | solution.py:114
  49.7 3.7 %collective-permute-start.10 = (bf16[256,512]{1,0:T(8,128)(2,1)S(1)}, bf16[256,512]{1,0:T(8,128)(2,1)S(1)}, u32[]{:S(2)}, u32[]{:S(2)}) collective-permute-start(bf16[256,512]{1,0:T(8,128)(2,1)S(1)} %collective-permute-done.9.refs_2_), channel_id=1, source_target_pairs={{1,0},{0,1},{3,2},{2,3},{5,4},{4,5},{7,6},{6,7},{9,8},{8,9},{11,10... | collective-permute-start | bytes 786440 | tf_op jit(solution)/shard_map/ppermute | solution.py:114
  53.2 7.2 %collective-permute-start.18 = (f16[256,128]{1,0:T(8,128)(2,1)S(1)}, f16[256,128]{1,0:T(8,128)(2,1)S(1)}, u32[]{:S(2)}, u32[]{:S(2)}) collective-permute-start(f16[256,128]{1,0:T(8,128)(2,1)S(1)} %fusion.3), channel_id=1, source_target_pairs={{8,0},{12,4},{0,8},{4,12},{9,1},{13,5},{1,9},{5,13},{10,2},{14,6},... | collective-permute-start | bytes 196616 | tf_op jit(solution)/shard_map/ppermute | solution.py:114
  53.3 7.7 %collective-permute-start.20 = (f16[256,128]{1,0:T(8,128)(2,1)S(1)}, f16[256,128]{1,0:T(8,128)(2,1)S(1)}, u32[]{:S(2)}, u32[]{:S(2)}) collective-permute-start(f16[256,128]{1,0:T(8,128)(2,1)S(1)} %fusion.5), channel_id=1, source_target_pairs={{12,0},{0,4},{4,8},{8,12},{13,1},{1,5},{5,9},{9,13},{14,2},{2,6},{... | collective-permute-start | bytes 196616 | tf_op jit(solution)/shard_map/ppermute | solution.py:114
  54.9 6.2 %copy-start.3 = (f32[256,64]{1,0:T(8,128)S(1)}, f32[256,64]{1,0:T(8,128)}, u32[]{:S(2)}) copy-start(f32[256,64]{1,0:T(8,128)} %get-tuple-element.14) | copy-start | bytes 196612
  54.9 6.2 %copy-start.4 = (f32[256,64]{1,0:T(8,128)S(1)}, f32[256,64]{1,0:T(8,128)}, u32[]{:S(2)}) copy-start(f32[256,64]{1,0:T(8,128)} %get-tuple-element.15) | copy-start | bytes 196612
  54.9 9.0 %copy-start.6 = (s32[8]{0:T(128)S(1)}, s32[8]{0:T(128)}, u32[]{:S(2)}) copy-start(s32[8]{0:T(128)} %param.9) | copy-start | bytes 100
  54.9 6.0 %collective-permute-start.19 = (f16[256,128]{1,0:T(8,128)(2,1)S(1)}, f16[256,128]{1,0:T(8,128)(2,1)S(1)}, u32[]{:S(2)}, u32[]{:S(2)}) collective-permute-start(f16[256,128]{1,0:T(8,128)(2,1)S(1)} %fusion.4), channel_id=1, source_target_pairs={{4,0},{8,4},{12,8},{0,12},{5,1},{9,5},{13,9},{1,13},{6,2},{10,6},{... | collective-permute-start | bytes 196616 | tf_op jit(solution)/shard_map/ppermute | solution.py:114
  57.1 31.3 %copy-start.2 = (f32[256,512]{1,0:T(8,128)S(1)}, f32[256,512]{1,0:T(8,128)}, u32[]{:S(2)}) copy-start(f32[256,512]{1,0:T(8,128)} %fusion.11) | copy-start | bytes 1572868
  57.1 31.3 %collective-permute-start.5 = (f16[256,512]{1,0:T(8,128)(2,1)S(1)}, f16[256,512]{1,0:T(8,128)(2,1)S(1)}, u32[]{:S(2)}, u32[]{:S(2)}) collective-permute-start(f16[256,512]{1,0:T(8,128)(2,1)S(1)} %fusion), channel_id=1, source_target_pairs={{8,0},{12,4},{0,8},{4,12},{9,1},{13,5},{1,9},{5,13},{10,2},{14,6},... | collective-permute-start | bytes 786440 | tf_op jit(solution)/shard_map/ppermute | solution.py:114
  59.5 28.9 %collective-permute-start.17 = (f16[256,512]{1,0:T(8,128)(2,1)S(1)}, f16[256,512]{1,0:T(8,128)(2,1)S(1)}, u32[]{:S(2)}, u32[]{:S(2)}) collective-permute-start(f16[256,512]{1,0:T(8,128)(2,1)S(1)} %fusion.2), channel_id=1, source_target_pairs={{12,0},{0,4},{4,8},{8,12},{13,1},{1,5},{5,9},{9,13},{14,2},{2,6},{... | collective-permute-start | bytes 786440 | tf_op jit(solution)/shard_map/ppermute | solution.py:114
  60.4 28.0 %collective-permute-start.11 = (f16[256,512]{1,0:T(8,128)(2,1)S(1)}, f16[256,512]{1,0:T(8,128)(2,1)S(1)}, u32[]{:S(2)}, u32[]{:S(2)}) collective-permute-start(f16[256,512]{1,0:T(8,128)(2,1)S(1)} %fusion.1), channel_id=1, source_target_pairs={{4,0},{8,4},{12,8},{0,12},{5,1},{9,5},{13,9},{1,13},{6,2},{10,6},{... | collective-permute-start | bytes 786440 | tf_op jit(solution)/shard_map/ppermute | solution.py:114
  61.3 12.1 %collective-permute-start.22 = (bf16[256,128]{1,0:T(8,128)(2,1)S(1)}, bf16[256,128]{1,0:T(8,128)(2,1)S(1)}, u32[]{:S(2)}, u32[]{:S(2)}) collective-permute-start(bf16[256,128]{1,0:T(8,128)(2,1)S(1)} %get-tuple-element.5), channel_id=1, source_target_pairs={{0,4},{4,8},{8,12},{1,5},{5,9},{9,13},{2,6},{6,10},{10,14},{3,7},{... | collective-permute-start | bytes 196616 | tf_op jit(solution)/shard_map/ppermute | solution.py:222
  62.6 24.8 %collective-permute-start.21 = (bf16[256,128]{1,0:T(8,128)(2,1)S(1)}, bf16[256,128]{1,0:T(8,128)(2,1)S(1)}, u32[]{:S(2)}, u32[]{:S(2)}) collective-permute-start(bf16[256,128]{1,0:T(8,128)(2,1)S(1)} %get-tuple-element.5), channel_id=1, source_target_pairs={{0,8},{4,12},{1,9},{5,13},{2,10},{6,14},{3,11},{7,15},{16,24},{20,... | collective-permute-start | bytes 196616 | tf_op jit(solution)/shard_map/ppermute | solution.py:222
  87.5 2.0 %collective-permute-start.23 = (bf16[768,128]{1,0:T(8,128)(2,1)S(1)}, bf16[768,128]{1,0:T(8,128)(2,1)S(1)}, u32[]{:S(2)}, u32[]{:S(2)}) collective-permute-start(bf16[768,128]{1,0:T(8,128)(2,1)S(1)} %pad_maximum_fusion.half_ref), channel_id=1, source_target_pairs={{1,0},{0,1},{3,2},{2,3},{5,4},{4,5},{7,6},{6,7},{9,8},{8,9},{11,10... | collective-permute-start | bytes 589832 | tf_op jit(solution)/shard_map/ppermute | solution.py:114
